TPU v7x, 32 devices: a whole 2x2x4 slice. The times are simulated.
32 devices in a mesh: tracts: 2 (over y), sky: 4 (over z), depth: 4 (over x, core).
Axes of the slice: x: 2, y: 2, z: 4, core: 2. Of those that a mesh axis runs over, the one named last changes fastest.
Arguments:
- visit_tiles: bfloat16 [128, 4, 64, 512], P(('tracts', 'sky', 'depth')), parts along dimension 0, may hold values from -6 to 6
- warp_matrix: bfloat16 [128, 512, 512], P(('tracts', 'sky', 'depth')), parts along dimension 0, may hold values from -0.25 to 0.25
- flux_scale: float32 [128], P(('tracts', 'sky', 'depth')), parts along dimension 0, may hold values from 0.3 to 3
- patch_lists: int32 [128, 4], P(('tracts', 'sky', 'depth')), parts along dimension 0, may hold values from 0 to 15, all different within a row; in each aligned block of 4 rows (0 to 3, 4 to 7, ...) at most 2 rows name the same one
- clip_bits: int32 [128, 4, 4, 512], P(('tracts', 'sky', 'depth')), parts along dimension 0, may hold values from -2147483648 to 2147483647, as said below
Outputs:
- coadd_mean: float32 [2, 32, 64, 512], P(None, ('tracts', 'sky'), 'depth'), parts along dimension 1
- coadd_var: float32 [2, 32, 64, 512], P(None, ('tracts', 'sky'), 'depth'), parts along dimension 1
There are 2 independent parts, one for each index of `tracts`. A program takes and returns all parts, laid end to end along the dimension named above; each array names one. Nothing has to cross between parts.
Inputs may be any that keep to these rules, and one draw needn't show every extreme that they name: `patch_lists`: row v names the 4 different patches of visit v's blocks. In the rows of one device no patch is named more than 2 times, a bound that some block reaches there; every patch is named by some row. Bit 16 t + j of clip_bits[v, k, g, c] is 1 when clip pass t (t = 0 or 1) keeps the sample of visit v's block k at row 16 g + j, column c.
All inputs are finite; a program needn't handle non-finite values.
Results may differ from a plain program's by a relative error of at most 0.0029.
Values may be sent and summed in bfloat16 or wider, within the bound.
A program may use at most 128 MiB of HBM per device.

v0:
```python
import functools

import jax
import jax.numpy as jnp
from jax import lax
from jax.experimental import pallas as pl
from jax.experimental.pallas import tpu as pltpu
from jax.sharding import PartitionSpec as P

PATCH_DEV = 4
CAPACITY = 2
SLOTS = PATCH_DEV * CAPACITY
MESH = pl.DeviceIdType.MESH
STEP = 4
LAG = 3


def kernel(sky, depth, scale_ref, src_ref, tiles_ref, matrix_ref, bits_ref, mean_ref, var_ref,
           warped, send_t, send_b, recv_t, recv_b, acc, st, sb, rt, rb):
    z, d = lax.axis_index("sky"), lax.axis_index("depth")
    me = z * depth + d
    devices = sky * depth
    visits, entries_rows, columns = tiles_ref.shape
    entries, rows, _ = warped.shape
    share = rows // depth

    def place(j):
        return lax.div(lax.rem(me + j, devices), depth), lax.rem(lax.rem(me + j, devices), depth)

    barrier = pltpu.get_barrier_semaphore()

    def greet(j, _):
        zz, dd = place(j)
        pl.semaphore_signal(barrier, inc=1, device_id={"sky": zz, "depth": dd}, device_id_type=MESH)
        return 0

    lax.fori_loop(1, devices, greet, 0)

    per_visit = entries // visits
    for v in range(visits):
        def warp(i, _, v=v):
            start = pl.multiple_of(i * STEP * rows, STEP * rows)
            product = jnp.dot(tiles_ref[v, pl.ds(start, STEP * rows), :], matrix_ref[v],
                              preferred_element_type=jnp.float32) * scale_ref[v]
            warped[pl.ds(v * per_visit + i * STEP, STEP)] = product.astype(jnp.bfloat16).reshape(STEP, rows, columns)
            return 0
        lax.fori_loop(0, per_visit // STEP, warp, 0)

    pl.semaphore_wait(barrier, devices - 1)

    def copies(zz, dd, there, mine):
        to = {"sky": zz, "depth": dd}
        return (
            pltpu.make_async_remote_copy(src_ref=send_t.at[there], dst_ref=recv_t.at[mine], send_sem=st.at[there],
                                         recv_sem=rt.at[mine], device_id=to, device_id_type=MESH),
            pltpu.make_async_remote_copy(src_ref=send_b.at[there], dst_ref=recv_b.at[mine], send_sem=sb.at[there],
                                         recv_sem=rb.at[mine], device_id=to, device_id_type=MESH),
        )

    def post(jj, _):
        zz = lax.rem(z + sky // 2 + jj, sky)

        def fill(s, _):
            e = src_ref[zz * SLOTS + s]
            valid = (e < entries).astype(jnp.int32)
            e = jnp.minimum(e, entries - 1)
            block = warped[e]
            flags = bits_ref[e] * valid
            for dd in range(depth):
                send_t[zz * depth + dd, s] = block[dd * share:(dd + 1) * share]
                send_b[zz * depth + dd, s] = flags[dd * (share // 16):(dd + 1) * (share // 16)]
            return 0

        lax.fori_loop(0, SLOTS, fill, 0)

        def start(k, _):
            dd = lax.rem(d + k, depth)
            there = zz * depth + dd

            @pl.when(there != me)
            def _():
                for c in copies(zz, dd, there, me):
                    c.start()
            return 0

        lax.fori_loop(0, depth, start, 0)
        return 0

    lax.fori_loop(0, sky, post, 0)

    acc[...] = jnp.zeros_like(acc)
    position = lax.rem(lax.broadcasted_iota(jnp.int32, (share, columns), 0), 16)

    def add(tiles, flags, source):
        for p in range(PATCH_DEV):
            sums = [acc[p, q] for q in range(6)]
            for c in range(CAPACITY):
                w = tiles[source, p * CAPACITY + c].astype(jnp.float32)
                packed = flags[source, p * CAPACITY + c]
                packed = jnp.broadcast_to(packed[:, None, :], (share // 16, 16, columns)).reshape(share, columns)
                shifted = lax.shift_right_logical(packed, position)
                first = (shifted & 1).astype(jnp.float32)
                both = first * (lax.shift_right_logical(shifted, 16) & 1).astype(jnp.float32)
                fw, bw = first * w, both * w
                for q, term in enumerate((first, fw, fw * w, both, bw, bw * w)):
                    sums[q] = sums[q] + term
            for q in range(6):
                acc[p, q] = sums[q]

    add(send_t, send_b, me)

    def take(jj, _):
        zz = lax.rem(z - sky // 2 - jj + 2 * sky, sky)

        def one(k, _):
            dd = lax.rem(d - k + depth, depth)
            there = zz * depth + dd

            @pl.when(there != me)
            def _():
                for c in copies(zz, dd, there, there):
                    c.wait_recv()
                add(recv_t, recv_b, there)
            return 0

        lax.fori_loop(0, depth, one, 0)
        return 0

    lax.fori_loop(0, sky, take, 0)

    for p in range(PATCH_DEV):
        cf, sf, qf, cb, sb_, qb = [acc[p, q] for q in range(6)]
        mean = sf / jnp.maximum(cf, 1.0)
        shift = sb_ - mean * cb
        square = qb - mean * sb_ - mean * shift
        step = shift / jnp.maximum(cb, 1.0)
        mean_ref[0, p] = mean
        mean_ref[1, p] = mean + step
        var_ref[0, p] = (qf - sf * mean) / jnp.maximum(cf - 1.0, 1.0)
        var_ref[1, p] = (square - shift * step) / jnp.maximum(cb - 1.0, 1.0)

    def drain(j, _):
        zz, dd = place(j)
        for c in copies(zz, dd, zz * depth + dd, me):
            c.wait_send()
        return 0

    lax.fori_loop(1, devices, drain, 0)


def folded(depth, scale_ref, src_ref, tiles_hbm, matrix_hbm, bits_hbm, out_ref,
           tiles_ref, matrix_ref, bits_ref, s_in,
           out_t, out_b, row_t, row_b, row_s, raw_t, raw_b, raw_s, far32, far16, got32, got16, tables, local,
           work_t, work_b,
           s_xt, r_xt, s_xb, r_xb, s_xs, r_xs, s_rt, r_rt, s_rb, r_rb, s_rs, r_rs, s_f, r_f, s_h, r_h, s_l):
    z, d = lax.axis_index("sky"), lax.axis_index("depth")
    half = z // 2
    rem = z - 2 * half
    inner, outer = rem != half, rem == half
    mate = 2 * half + 1 - rem
    across, beyond = 3 - z, 3 - mate
    parts, _, entries, slab, width = out_t.shape
    groups_here = out_b.shape[0] * width // tiles_ref.shape[2]
    visits, entries_rows, columns = tiles_ref.shape
    per_visit = entries // visits
    rows = entries_rows // per_visit
    share = rows // depth
    slabs = share // slab

    bands = matrix_ref.shape[0]
    tiles_in = pltpu.make_async_copy(tiles_hbm, tiles_ref, s_in.at[bands])
    bits_in = pltpu.make_async_copy(bits_hbm, bits_ref, s_in.at[bands + 1])

    def matrix_in(band):
        lanes = pl.ds(band * width, width)
        return pltpu.make_async_copy(matrix_hbm.at[:, :, lanes], matrix_ref.at[band], s_in.at[band])

    tiles_in.start()
    matrix_in(0).start()
    bits_in.start()
    for band in range(1, bands):
        matrix_in(band).start()

    barrier = pltpu.get_barrier_semaphore()
    for k in range(1, 4):
        pl.semaphore_signal(barrier, inc=1, device_id={"sky": lax.rem(z + k, 4)}, device_id_type=MESH)
    for k in range(1, depth):
        pl.semaphore_signal(barrier, inc=1, device_id={"depth": lax.rem(d + k, depth)}, device_id_type=MESH)

    def remote(src, dst, send, recv, to):
        return pltpu.make_async_remote_copy(src_ref=src, dst_ref=dst, send_sem=send, recv_sem=recv, device_id=to,
                                            device_id_type=MESH)

    def to_row(c, there, slot):
        to = {"depth": there}
        return remote(out_t.at[c, there], row_t.at[c, slot], s_xt.at[c, there], r_xt.at[c, slot], to)

    def flags_to_row(b, there, slot):
        to = {"depth": there}
        return remote(out_b.at[b, there], row_b.at[b, slot], s_xb.at[b, there], r_xb.at[b, slot], to)

    def table_to_row(there, slot):
        return remote(src_ref, row_s.at[slot], s_xs.at[there], r_xs.at[slot], {"depth": there})

    def to_mate(c):
        to = {"sky": mate}
        return remote(row_t.at[c], raw_t.at[c], s_rt.at[c], r_rt.at[c], to)

    def flags_to_mate(b):
        return remote(row_b.at[b], raw_b.at[b], s_rb.at[b], r_rb.at[b], {"sky": mate})

    def table_to_mate():
        return remote(row_s, raw_s, s_rs.at[0], r_rs.at[0], {"sky": mate})

    def sums_to(c, t, where, slot):
        to = {"sky": where}
        return (remote(far32.at[c, t], got32.at[c, slot], s_f.at[c, t], r_f.at[c, slot], to),
                remote(far16.at[c, t], got16.at[c, slot], s_h.at[c, t], r_h.at[c, slot], to))

    position = lax.broadcasted_iota(jnp.int32, (slab, width), 0)
    work_t[...] = jnp.zeros_like(work_t)
    work_b[...] = jnp.zeros_like(work_b)

    def stage(c, which, tiles, flags):
        work_t[which, :, :entries] = tiles[c]
        work_b[which, :, :entries] = flags[c // 2]

    def gather(c, patch, groups):
        place = position + (c % 2) * slab
        sums = [jnp.zeros((slab, width), jnp.float32)] * 6
        for which in range(groups):
            for dd in range(depth):
                for k in range(CAPACITY):
                    e = tables[which, dd, 0, patch * CAPACITY + k]
                    w = work_t[which, dd, e].astype(jnp.float32)
                    packed = jnp.broadcast_to(work_b[which, dd, e], (slab, width))
                    shifted = lax.shift_right_logical(packed, place)
                    first = (shifted & 1).astype(jnp.float32)
                    both = first * (lax.shift_right_logical(shifted, 16) & 1).astype(jnp.float32)
                    fw, bw = first * w, both * w
                    sums = [a + b for a, b in zip(sums, (first, fw, fw * w, both, bw, bw * w))]
        return sums

    def send_sums(c, t, where, groups):
        def one(p, _):
            cf, sf, qf, cb, sb, qb = gather(c, where * PATCH_DEV + p, groups)
            for q, value in enumerate((sf, qf, sb, qb)):
                far32[c, t, p, q] = value
            for q, value in enumerate((cf, cb)):
                far16[c, t, p, q] = value.astype(jnp.bfloat16)
            return 0
        lax.fori_loop(0, PATCH_DEV, one, 0)
        for copy in sums_to(c, t, where, half):
            copy.start()

    def warp(column, _):
        lanes = pl.ds(pl.multiple_of(column * width, width), width)
        for band in range(bands):
            @pl.when(column == band)
            def _(band=band):
                matrix_in(band).wait()
        for v in range(visits):
            product = jnp.dot(tiles_ref[v], matrix_ref[column, v], preferred_element_type=jnp.float32)
            block = (product * scale_ref[v]).reshape(per_visit, depth, slabs, slab, width)
            for dd in range(depth):
                for h in range(slabs):
                    out_t[column * slabs + h, dd, v * per_visit:(v + 1) * per_visit] = block[:, dd, h].astype(jnp.bfloat16)
        for g in range(groups_here):
            b = column * groups_here + g
            for dd in range(depth):
                line = dd * groups_here + g
                out_b[b, dd] = bits_ref[:, line:line + 1, lanes]
            row_b[b, d] = out_b[b, d]
        for h in range(slabs):
            row_t[column * slabs + h, d] = out_t[column * slabs + h, d]

        @pl.when(column == 0)
        def _():
            pl.semaphore_wait(barrier, 3 + depth - 1)
            for k in range(1, depth):
                table_to_row(lax.rem(d + k, depth), d).start()

        for h in range(slabs):
            for k in range(1, depth):
                there = lax.rem(d + k, depth)
                if h % 2 == 0:
                    flags_to_row(column * groups_here + h // 2, there, d).start()
                to_row(column * slabs + h, there, d).start()
        return 0

    tiles_in.wait()
    bits_in.wait()
    lax.fori_loop(0, bands, warp, 0)
    row_s[d] = src_ref[...]
    mine, theirs = (row_t, row_b), (raw_t, raw_b)

    for k in range(1, depth):
        table_to_row(lax.rem(d + k, depth), lax.rem(d + depth - k, depth)).wait_recv()
    held = pltpu.make_async_copy(row_s, tables.at[0], s_l.at[0])
    held.start()

    @pl.when(outer)
    def _():
        table_to_mate().start()

    held.wait()

    def total(c, slot, p):
        sf, qf, sb, qb = [got32[c, slot, p, q] for q in range(4)]
        cf, cb = [got16[c, slot, p, q].astype(jnp.float32) for q in range(2)]
        return cf, sf, qf, cb, sb, qb

    def finish(c):
        lanes = pl.ds(pl.multiple_of(c // slabs * width, width), width)
        lines = pl.ds(pl.multiple_of(c % slabs * slab, slab), slab)
        stage(c, 0, *mine)

        @pl.when(inner)
        def _():
            stage(c, 1, *theirs)

            def one(p, _):
                for q, value in enumerate(gather(c, z * PATCH_DEV + p, 2)):
                    local[p, q] = value
                return 0
            lax.fori_loop(0, PATCH_DEV, one, 0)

        @pl.when(outer)
        def _():
            def one(p, _):
                for q, value in enumerate(gather(c, z * PATCH_DEV + p, 1)):
                    local[p, q] = value
                return 0
            lax.fori_loop(0, PATCH_DEV, one, 0)
            for copy in sums_to(c, 2, mate, half):
                copy.wait_recv()
            for p in range(PATCH_DEV):
                for q, value in enumerate(total(c, half, p)):
                    local[p, q] = local[p, q] + value

        for copy in sums_to(c, 0, across, 1 - half):
            copy.wait_recv()
        for p in range(PATCH_DEV):
            cf, sf, qf, cb, sb, qb = [local[p, q] + value for q, value in enumerate(total(c, 1 - half, p))]
            mean = sf / jnp.maximum(cf, 1.0)
            shift = sb - mean * cb
            square = qb - mean * sb - mean * shift
            step = shift / jnp.maximum(cb, 1.0)
            out_ref[0, 0, p, lines, lanes] = mean
            out_ref[0, 1, p, lines, lanes] = mean + step
            out_ref[1, 0, p, lines, lanes] = (qf - sf * mean) / jnp.maximum(cf - 1.0, 1.0)
            out_ref[1, 1, p, lines, lanes] = (square - shift * step) / jnp.maximum(cb - 1.0, 1.0)

    def forward(c, _):
        fresh = c % 2 == 0
        b = c // 2

        @pl.when(fresh)
        def _():
            for k in range(1, depth):
                flags_to_row(b, lax.rem(d + k, depth), lax.rem(d + depth - k, depth)).wait_recv()

        for k in range(1, depth):
            to_row(c, lax.rem(d + k, depth), lax.rem(d + depth - k, depth)).wait_recv()

        @pl.when(outer)
        def _():
            @pl.when(fresh)
            def _():
                flags_to_mate(b).start()
            to_mate(c).start()

        @pl.when(inner)
        def _():
            stage(c, 0, *mine)
            send_sums(c, 2, mate, 1)

            @pl.when(c == 0)
            def _():
                table_to_mate().wait_recv()
                other = pltpu.make_async_copy(raw_s, tables.at[1], s_l.at[1])
                other.start()
                other.wait()

            @pl.when(fresh)
            def _():
                flags_to_mate(b).wait_recv()

            to_mate(c).wait_recv()
            stage(c, 1, *theirs)
            send_sums(c, 0, beyond, 2)
            send_sums(c, 1, across, 2)

            @pl.when(c >= LAG)
            def _():
                finish(c - LAG)
        return 0

    lax.fori_loop(0, parts, forward, 0)

    def close(c, _):
        @pl.when(jnp.logical_or(outer, c >= parts - LAG))
        def _():
            finish(c)
        return 0

    lax.fori_loop(0, parts, close, 0)

    for k in range(1, depth):
        table_to_row(lax.rem(d + k, depth), d).wait_send()

    @pl.when(outer)
    def _():
        table_to_mate().wait_send()

    def drain_flags(b, _):
        for k in range(1, depth):
            flags_to_row(b, lax.rem(d + k, depth), d).wait_send()

        @pl.when(outer)
        def _():
            flags_to_mate(b).wait_send()
        return 0

    lax.fori_loop(0, parts // 2, drain_flags, 0)

    def drain(c, _):
        for k in range(1, depth):
            to_row(c, lax.rem(d + k, depth), d).wait_send()

        @pl.when(outer)
        def _():
            to_mate(c).wait_send()

        @pl.when(inner)
        def _():
            for t, where in ((0, beyond), (1, across), (2, mate)):
                for copy in sums_to(c, t, where, half):
                    copy.wait_send()
        return 0

    lax.fori_loop(0, parts, drain, 0)


def split(both_ref, mean_ref, var_ref):
    mean_ref[...] = both_ref[0]
    var_ref[...] = both_ref[1]


def per_device(sky, depth, visit_tiles, warp_matrix, flux_scale, patch_lists, clip_bits):
    visits, own, rows, columns = visit_tiles.shape
    entries = visits * own
    patches = PATCH_DEV * sky
    devices = sky * depth
    share = rows // depth
    targets = patch_lists.reshape(entries)
    number = jnp.arange(entries, dtype=jnp.int32)
    same = (targets[:, None] == targets[None, :]) & (number[None, :] < number[:, None])
    rank = jnp.sum(same.astype(jnp.int32), axis=1)
    slot = targets * CAPACITY + rank
    source = jnp.min(
        jnp.where(slot[None, :] == jnp.arange(patches * CAPACITY, dtype=jnp.int32)[:, None], number[None, :], entries),
        axis=1,
    )
    smem, vmem = pl.BlockSpec(memory_space=pltpu.SMEM), pl.BlockSpec(memory_space=pltpu.VMEM)
    hbm = pl.BlockSpec(memory_space=pltpu.HBM)
    out = jax.ShapeDtypeStruct((2, PATCH_DEV, share, columns), jnp.float32)
    if sky == 4:
        width = 128
        slab = 8
        parts = columns // width * (share // slab)
        long = -(-patches * CAPACITY // 128) * 128
        table = jnp.pad(source, (0, long - patches * CAPACITY), constant_values=entries)[None, :]
        blocks = (parts, depth, entries, slab, width)
        flags = (parts // 2, depth, entries, 1, width)
        work = (2, depth, entries + 1)
        dma = pltpu.SemaphoreType.DMA
        both = pl.pallas_call(
            functools.partial(folded, depth),
            out_shape=jax.ShapeDtypeStruct((2,) + out.shape, jnp.float32),
            in_specs=[smem, vmem, hbm, hbm, hbm],
            out_specs=vmem,
            scratch_shapes=[
                pltpu.VMEM((visits, own * rows, columns), jnp.bfloat16),
                pltpu.VMEM((columns // width, visits, columns, width), jnp.bfloat16),
                pltpu.VMEM((entries, rows // 16, columns), jnp.int32),
                dma((columns // width + 2,)),
                pltpu.VMEM(blocks, jnp.bfloat16), pltpu.VMEM(flags, jnp.int32),
                pltpu.VMEM(blocks, jnp.bfloat16), pltpu.VMEM(flags, jnp.int32), pltpu.VMEM((depth, 1, long), jnp.int32),
                pltpu.VMEM(blocks, jnp.bfloat16), pltpu.VMEM(flags, jnp.int32), pltpu.VMEM((depth, 1, long), jnp.int32),
                pltpu.VMEM((parts, 3, PATCH_DEV, 4, slab, width), jnp.float32),
                pltpu.VMEM((parts, 3, PATCH_DEV, 2, slab, width), jnp.bfloat16),
                pltpu.VMEM((parts, 2, PATCH_DEV, 4, slab, width), jnp.float32),
                pltpu.VMEM((parts, 2, PATCH_DEV, 2, slab, width), jnp.bfloat16),
                pltpu.SMEM((2, depth, 1, long), jnp.int32),
                pltpu.VMEM((PATCH_DEV, 6, slab, width), jnp.float32),
                pltpu.VMEM(work + blocks[3:], jnp.bfloat16), pltpu.VMEM(work + flags[3:], jnp.int32),
                dma((parts, depth)), dma((parts, depth)), dma((parts // 2, depth)), dma((parts // 2, depth)),
                dma((depth,)), dma((depth,)),
                dma((parts,)), dma((parts,)), dma((parts // 2,)), dma((parts // 2,)), dma((1,)), dma((1,)),
                dma((parts, 3)), dma((parts, 2)), dma((parts, 3)), dma((parts, 2)), dma((2,)),
            ],
            compiler_params=pltpu.CompilerParams(
                collective_id=0, has_side_effects=True, vmem_limit_bytes=67043328 - 1048576
            ),
        )(flux_scale, table, visit_tiles.reshape(visits, own * rows, columns), warp_matrix,
          clip_bits.reshape(entries, rows // 16, columns))
        return pl.pallas_call(
            split, out_shape=(out, out), in_specs=[vmem], out_specs=(vmem, vmem),
            compiler_params=pltpu.CompilerParams(vmem_limit_bytes=67043328 - 1048576),
        )(both)
    return pl.pallas_call(
        functools.partial(kernel, sky, depth),
        out_shape=(out, out),
        in_specs=[smem, smem, vmem, vmem, vmem],
        out_specs=(vmem, vmem),
        scratch_shapes=[
            pltpu.VMEM((entries, rows, columns), jnp.bfloat16),
            pltpu.VMEM((devices, SLOTS, share, columns), jnp.bfloat16),
            pltpu.VMEM((devices, SLOTS, share // 16, columns), jnp.int32),
            pltpu.VMEM((devices, SLOTS, share, columns), jnp.bfloat16),
            pltpu.VMEM((devices, SLOTS, share // 16, columns), jnp.int32),
            pltpu.VMEM((PATCH_DEV, 6, share, columns), jnp.float32),
        ] + [pltpu.SemaphoreType.DMA((devices,))] * 4,
        compiler_params=pltpu.CompilerParams(
            collective_id=0, has_side_effects=True, vmem_limit_bytes=67043328 - 1048576
        ),
    )(flux_scale, source, visit_tiles.reshape(visits, own * rows, columns), warp_matrix,
      clip_bits.reshape(entries, rows // 16, columns))


def solution(mesh):
    whole = ("tracts", "sky", "depth")
    placed = (P(whole, None, None, None), P(whole, None, None), P(whole), P(whole, None), P(whole, None, None, None))
    outs = P(None, ("tracts", "sky"), "depth", None)
    return jax.shard_map(
        functools.partial(per_device, mesh.shape["sky"], mesh.shape["depth"]),
        mesh=mesh,
        in_specs=placed,
        out_specs=(outs, outs),
        check_vma=False,
    )
```

profile of v0, /device:TPU:0, one launch (start us, length us, event | category | flops | bytes accessed | tf_op | source)
XLA Modules:
  0.0 52.3 jit_solution(9808123544425631108)
XLA Ops:
  0.6 0.8 %reshape.23 = s32[16]{0:T(128)S(1)} reshape(s32[4,4]{1,0:T(4,128)} %param.8) | data formatting | bytes 128 | tf_op jit(solution)/shard_map/reshape | solution.py:456
  1.4 0.2 convert_reduce_fusion
  1.6 0.1 select_reduce_fusion
  1.7 0.5 pad_bitcast_fusion.src_ref
  2.2 48.2 %shard_map.68.both_ref = f32[2,2,4,16,512]{4,3,2,1,0:T(8,128)} custom-call(f32[4]{0:T(128)} %scale_ref.1, s32[1,128]{1,0:T(1,128)} %pad_bitcast_fusion.src_ref, bf16[4,256,512]{2,1,0:T(8,128)(2,1)} %bitcast.4, bf16[4,512,512]{2,1,0:T(8,128)(2,1)} %matrix_hbm.1, s32[16,4,512]{2,1,0:T(4,128)} %bitcast.5), custom_call_target="tpu_custom_call" | custom-call | tf_op jit(solution)/shard_map/pallas_call | solution.py:478
  50.5 1.8 %shard_map.69 = (f32[2,4,16,512]{3,2,1,0:T(8,128)}, f32[2,4,16,512]{3,2,1,0:T(8,128)}) custom-call(f32[2,2,4,16,512]{4,3,2,1,0:T(8,128)} %shard_map.68.both_ref), custom_call_target="tpu_custom_call" | custom-call | tf_op jit(solution)/shard_map/pallas_call | solution.py:508
  (1 shorter events, 0.0 us)
where the time goes:
time: 52.5 us; the launch traced here: 52.3 us
  Pallas kernels  50.1 us (95%)
  local copies, waits for them, and re-layouts  1.28 us (2%)
  between operations  0.64 us (1%)
    pallas_call x1, Pallas kernels, per_device(): pl.pallas_call(functools.partial(folded, depth), out_shape=jax.ShapeDtype...  48.2 us
    pallas_call x1, Pallas kernels, per_device(): pl.pallas_call(split, out_shape=(out, out), in_specs=[vmem], out_specs=(v...  1.85 us

commit v1 on v0

--- a/solution.py
+++ b/solution.py
@@ -13,6 +13,7 @@
 MESH = pl.DeviceIdType.MESH
 STEP = 4
 LAG = 3
+LEAD = 2
 
 
 def kernel(sky, depth, scale_ref, src_ref, tiles_ref, matrix_ref, bits_ref, mean_ref, var_ref,
@@ -148,17 +149,20 @@
     lax.fori_loop(1, devices, drain, 0)
 
 
-def folded(depth, scale_ref, src_ref, tiles_hbm, matrix_hbm, bits_hbm, out_ref,
-           tiles_ref, matrix_ref, bits_ref, s_in,
-           out_t, out_b, row_t, row_b, row_s, raw_t, raw_b, raw_s, far32, far16, got32, got16, tables, local,
+def folded(depth, scale_hbm, lists_hbm, tiles_hbm, matrix_hbm, bits_hbm, out_ref,
+           scale_ref, lists_ref, tiles_ref, matrix_ref, bits_ref, s_in,
+           out_t, out_b, row_t, row_b, raw_t, raw_b, own_s, row_s, raw_s, far32, far16, got32, got16, tables, local,
            work_t, work_b,
-           s_xt, r_xt, s_xb, r_xb, s_xs, r_xs, s_rt, r_rt, s_rb, r_rb, s_rs, r_rs, s_f, r_f, s_h, r_h, s_l):
+           s_xt, r_xt, s_xb, r_xb, s_xs, r_xs, s_ms, r_ms, s_dt, r_dt, s_db, r_db, s_ft, r_ft, s_fb, r_fb,
+           s_f, r_f, s_h, r_h, s_l):
     z, d = lax.axis_index("sky"), lax.axis_index("depth")
     half = z // 2
     rem = z - 2 * half
     inner, outer = rem != half, rem == half
     mate = 2 * half + 1 - rem
     across, beyond = 3 - z, 3 - mate
+    base = d // 2 * 2
+    other = depth - 2 - base
     parts, _, entries, slab, width = out_t.shape
     groups_here = out_b.shape[0] * width // tiles_ref.shape[2]
     visits, entries_rows, columns = tiles_ref.shape
@@ -166,27 +170,37 @@
     rows = entries_rows // per_visit
     share = rows // depth
     slabs = share // slab
+    long = own_s.shape[1]
 
     bands = matrix_ref.shape[0]
     tiles_in = pltpu.make_async_copy(tiles_hbm, tiles_ref, s_in.at[bands])
     bits_in = pltpu.make_async_copy(bits_hbm, bits_ref, s_in.at[bands + 1])
+    scale_in = pltpu.make_async_copy(scale_hbm, scale_ref, s_in.at[bands + 2])
+    lists_in = pltpu.make_async_copy(lists_hbm, lists_ref, s_in.at[bands + 3])
 
     def matrix_in(band):
         lanes = pl.ds(band * width, width)
         return pltpu.make_async_copy(matrix_hbm.at[:, :, lanes], matrix_ref.at[band], s_in.at[band])
 
+    barrier = pltpu.get_barrier_semaphore()
+    for k in range(1, depth):
+        pl.semaphore_signal(barrier, inc=1, device_id={"depth": lax.rem(d + k, depth)}, device_id_type=MESH)
+    for k in range(depth):
+        pl.semaphore_signal(barrier, inc=1, device_id={"sky": mate, "depth": k}, device_id_type=MESH)
+    pl.semaphore_signal(barrier, inc=1, device_id={"sky": beyond}, device_id_type=MESH)
+
+    @pl.when(inner)
+    def _():
+        pl.semaphore_signal(barrier, inc=1, device_id={"sky": across}, device_id_type=MESH)
+
     tiles_in.start()
     matrix_in(0).start()
+    lists_in.start()
+    scale_in.start()
     bits_in.start()
     for band in range(1, bands):
         matrix_in(band).start()
 
-    barrier = pltpu.get_barrier_semaphore()
-    for k in range(1, 4):
-        pl.semaphore_signal(barrier, inc=1, device_id={"sky": lax.rem(z + k, 4)}, device_id_type=MESH)
-    for k in range(1, depth):
-        pl.semaphore_signal(barrier, inc=1, device_id={"depth": lax.rem(d + k, depth)}, device_id_type=MESH)
-
     def remote(src, dst, send, recv, to):
         return pltpu.make_async_remote_copy(src_ref=src, dst_ref=dst, send_sem=send, recv_sem=recv, device_id=to,
                                             device_id_type=MESH)
@@ -200,17 +214,26 @@
         return remote(out_b.at[b, there], row_b.at[b, slot], s_xb.at[b, there], r_xb.at[b, slot], to)
 
     def table_to_row(there, slot):
-        return remote(src_ref, row_s.at[slot], s_xs.at[there], r_xs.at[slot], {"depth": there})
-
-    def to_mate(c):
-        to = {"sky": mate}
-        return remote(row_t.at[c], raw_t.at[c], s_rt.at[c], r_rt.at[c], to)
-
-    def flags_to_mate(b):
-        return remote(row_b.at[b], raw_b.at[b], s_rb.at[b], r_rb.at[b], {"sky": mate})
-
-    def table_to_mate():
-        return remote(row_s, raw_s, s_rs.at[0], r_rs.at[0], {"sky": mate})
+        return remote(own_s, row_s.at[slot], s_xs.at[there], r_xs.at[slot], {"depth": there})
+
+    def table_to_mates(there, slot):
+        return remote(own_s, raw_s.at[slot], s_ms.at[there], r_ms.at[slot], {"sky": mate, "depth": there})
+
+    def direct(c, there, slot):
+        to = {"sky": mate, "depth": there}
+        return remote(out_t.at[c, there], raw_t.at[c, slot], s_dt.at[c, there], r_dt.at[c, slot], to)
+
+    def flags_direct(b, there, slot):
+        to = {"sky": mate, "depth": there}
+        return remote(out_b.at[b, there], raw_b.at[b, slot], s_db.at[b, there], r_db.at[b, slot], to)
+
+    def onward(c, start):
+        pair = pl.ds(start, 2)
+        return remote(row_t.at[c, pair], raw_t.at[c, pair], s_ft.at[c], r_ft.at[c], {"sky": mate})
+
+    def flags_onward(b, start):
+        pair = pl.ds(start, 2)
+        return remote(row_b.at[b, pair], raw_b.at[b, pair], s_fb.at[b], r_fb.at[b], {"sky": mate})
 
     def sums_to(c, t, where, slot):
         to = {"sky": where}
@@ -218,8 +241,22 @@
                 remote(far16.at[c, t], got16.at[c, slot], s_h.at[c, t], r_h.at[c, slot], to))
 
     position = lax.broadcasted_iota(jnp.int32, (slab, width), 0)
-    work_t[...] = jnp.zeros_like(work_t)
-    work_b[...] = jnp.zeros_like(work_b)
+    for which in range(2):
+        for dd in range(depth):
+            work_t[which, dd, entries] = jnp.zeros((slab, width), jnp.bfloat16)
+            work_b[which, dd, entries] = jnp.zeros((1, width), jnp.int32)
+
+    lists_in.wait()
+    lane = lax.broadcasted_iota(jnp.int32, (1, long), 1)
+    table = jnp.full((1, long), entries, jnp.int32)
+    targets = [lists_ref[v, k] for v in range(visits) for k in range(per_visit)]
+    for e in range(entries):
+        rank = jnp.int32(0)
+        for f in range(e // per_visit * per_visit):
+            rank = rank + (targets[e] == targets[f]).astype(jnp.int32)
+        table = jnp.where(lane == targets[e] * CAPACITY + rank, e, table)
+    own_s[...] = table
+    row_s[d] = table
 
     def stage(c, which, tiles, flags):
         work_t[which, :, :entries] = tiles[c]
@@ -244,14 +281,23 @@
     def send_sums(c, t, where, groups):
         def one(p, _):
             cf, sf, qf, cb, sb, qb = gather(c, where * PATCH_DEV + p, groups)
-            for q, value in enumerate((sf, qf, sb, qb)):
-                far32[c, t, p, q] = value
-            for q, value in enumerate((cf, cb)):
+            mean = sf / jnp.maximum(cf, 1.0)
+            far32[c, t, p] = sf
+            packed = (cf, cb, qf - sf * mean, sb - mean * cb, qb - sb * (sb / jnp.maximum(cb, 1.0)))
+            for q, value in enumerate(packed):
                 far16[c, t, p, q] = value.astype(jnp.bfloat16)
             return 0
         lax.fori_loop(0, PATCH_DEV, one, 0)
         for copy in sums_to(c, t, where, half):
             copy.start()
+
+    def send_direct(c):
+        @pl.when(c % 2 == 0)
+        def _():
+            for j in range(2):
+                flags_direct(c // 2, base + j, d).start()
+        for j in range(2):
+            direct(c, base + j, d).start()
 
     def warp(column, _):
         lanes = pl.ds(pl.multiple_of(column * width, width), width)
@@ -276,9 +322,20 @@
 
         @pl.when(column == 0)
         def _():
-            pl.semaphore_wait(barrier, 3 + depth - 1)
+            @pl.when(inner)
+            def _():
+                pl.semaphore_wait(barrier, 2 * depth + 1)
+
+            @pl.when(outer)
+            def _():
+                pl.semaphore_wait(barrier, 2 * depth)
             for k in range(1, depth):
                 table_to_row(lax.rem(d + k, depth), d).start()
+
+            @pl.when(outer)
+            def _():
+                for k in range(depth):
+                    table_to_mates(k, d).start()
 
         for h in range(slabs):
             for k in range(1, depth):
@@ -286,29 +343,30 @@
                 if h % 2 == 0:
                     flags_to_row(column * groups_here + h // 2, there, d).start()
                 to_row(column * slabs + h, there, d).start()
+
+            @pl.when(jnp.logical_and(outer, column * slabs + h < LEAD))
+            def _(h=h):
+                send_direct(column * slabs + h)
         return 0
 
     tiles_in.wait()
+    scale_in.wait()
     bits_in.wait()
     lax.fori_loop(0, bands, warp, 0)
-    row_s[d] = src_ref[...]
     mine, theirs = (row_t, row_b), (raw_t, raw_b)
 
     for k in range(1, depth):
         table_to_row(lax.rem(d + k, depth), lax.rem(d + depth - k, depth)).wait_recv()
     held = pltpu.make_async_copy(row_s, tables.at[0], s_l.at[0])
     held.start()
-
-    @pl.when(outer)
-    def _():
-        table_to_mate().start()
-
     held.wait()
 
     def total(c, slot, p):
-        sf, qf, sb, qb = [got32[c, slot, p, q] for q in range(4)]
-        cf, cb = [got16[c, slot, p, q].astype(jnp.float32) for q in range(2)]
-        return cf, sf, qf, cb, sb, qb
+        sf = got32[c, slot, p]
+        cf, cb, mf, shift, mb = [got16[c, slot, p, q].astype(jnp.float32) for q in range(5)]
+        mean = sf / jnp.maximum(cf, 1.0)
+        sb = shift + mean * cb
+        return cf, sf, mf + sf * mean, cb, sb, mb + sb * (sb / jnp.maximum(cb, 1.0))
 
     def finish(c):
         lanes = pl.ds(pl.multiple_of(c // slabs * width, width), width)
@@ -367,8 +425,12 @@
         def _():
             @pl.when(fresh)
             def _():
-                flags_to_mate(b).start()
-            to_mate(c).start()
+                flags_onward(b, other).start()
+            onward(c, other).start()
+
+            @pl.when(c + LEAD < parts)
+            def _():
+                send_direct(c + LEAD)
 
         @pl.when(inner)
         def _():
@@ -377,16 +439,21 @@
 
             @pl.when(c == 0)
             def _():
-                table_to_mate().wait_recv()
-                other = pltpu.make_async_copy(raw_s, tables.at[1], s_l.at[1])
-                other.start()
-                other.wait()
+                for k in range(depth):
+                    table_to_mates(k, k).wait_recv()
+                more = pltpu.make_async_copy(raw_s, tables.at[1], s_l.at[1])
+                more.start()
+                more.wait()
 
             @pl.when(fresh)
             def _():
-                flags_to_mate(b).wait_recv()
-
-            to_mate(c).wait_recv()
+                for j in range(2):
+                    flags_direct(b, base + j, base + j).wait_recv()
+                flags_onward(b, other).wait_recv()
+
+            for j in range(2):
+                direct(c, base + j, base + j).wait_recv()
+            onward(c, other).wait_recv()
             stage(c, 1, *theirs)
             send_sums(c, 0, beyond, 2)
             send_sums(c, 1, across, 2)
@@ -411,7 +478,8 @@
 
     @pl.when(outer)
     def _():
-        table_to_mate().wait_send()
+        for k in range(depth):
+            table_to_mates(k, d).wait_send()
 
     def drain_flags(b, _):
         for k in range(1, depth):
@@ -419,7 +487,9 @@
 
         @pl.when(outer)
         def _():
-            flags_to_mate(b).wait_send()
+            for j in range(2):
+                flags_direct(b, base + j, d).wait_send()
+            flags_onward(b, other).wait_send()
         return 0
 
     lax.fori_loop(0, parts // 2, drain_flags, 0)
@@ -430,7 +500,9 @@
 
         @pl.when(outer)
         def _():
-            to_mate(c).wait_send()
+            for j in range(2):
+                direct(c, base + j, d).wait_send()
+            onward(c, other).wait_send()
 
         @pl.when(inner)
         def _():
@@ -442,9 +514,12 @@
     lax.fori_loop(0, parts, drain, 0)
 
 
-def split(both_ref, mean_ref, var_ref):
-    mean_ref[...] = both_ref[0]
-    var_ref[...] = both_ref[1]
+def split(both_ref, mean_hbm, var_hbm, sems):
+    copies = [pltpu.make_async_copy(both_ref.at[q], out, sems.at[q]) for q, out in enumerate((mean_hbm, var_hbm))]
+    for copy in copies:
+        copy.start()
+    for copy in copies:
+        copy.wait()
 
 
 def per_device(sky, depth, visit_tiles, warp_matrix, flux_scale, patch_lists, clip_bits):
@@ -453,6 +528,60 @@
     patches = PATCH_DEV * sky
     devices = sky * depth
     share = rows // depth
+    smem, vmem = pl.BlockSpec(memory_space=pltpu.SMEM), pl.BlockSpec(memory_space=pltpu.VMEM)
+    hbm = pl.BlockSpec(memory_space=pltpu.HBM)
+    out = jax.ShapeDtypeStruct((2, PATCH_DEV, share, columns), jnp.float32)
+    if sky == 4 and depth == 4:
+        width = 128
+        slab = 8
+        bands = columns // width
+        parts = bands * (share // slab)
+        long = -(-patches * CAPACITY // 128) * 128
+        blocks = (parts, depth, entries, slab, width)
+        flags = (parts // 2, depth, entries, 1, width)
+        work = (2, depth, entries + 1)
+        dma = pltpu.SemaphoreType.DMA
+        both = pl.pallas_call(
+            functools.partial(folded, depth),
+            out_shape=jax.ShapeDtypeStruct((2,) + out.shape, jnp.float32),
+            in_specs=[hbm] * 5,
+            out_specs=vmem,
+            scratch_shapes=[
+                pltpu.SMEM((visits,), jnp.float32),
+                pltpu.SMEM((visits, own), jnp.int32),
+                pltpu.VMEM((visits, own * rows, columns), jnp.bfloat16),
+                pltpu.VMEM((bands, visits, columns, width), jnp.bfloat16),
+                pltpu.VMEM((entries, rows // 16, columns), jnp.int32),
+                dma((bands + 4,)),
+                pltpu.VMEM(blocks, jnp.bfloat16), pltpu.VMEM(flags, jnp.int32),
+                pltpu.VMEM(blocks, jnp.bfloat16), pltpu.VMEM(flags, jnp.int32),
+                pltpu.VMEM(blocks, jnp.bfloat16), pltpu.VMEM(flags, jnp.int32),
+                pltpu.VMEM((1, long), jnp.int32),
+                pltpu.VMEM((depth, 1, long), jnp.int32), pltpu.VMEM((depth, 1, long), jnp.int32),
+                pltpu.VMEM((parts, 3, PATCH_DEV, slab, width), jnp.float32),
+                pltpu.VMEM((parts, 3, PATCH_DEV, 5, slab, width), jnp.bfloat16),
+                pltpu.VMEM((parts, 2, PATCH_DEV, slab, width), jnp.float32),
+                pltpu.VMEM((parts, 2, PATCH_DEV, 5, slab, width), jnp.bfloat16),
+                pltpu.SMEM((2, depth, 1, long), jnp.int32),
+                pltpu.VMEM((PATCH_DEV, 6, slab, width), jnp.float32),
+                pltpu.VMEM(work + blocks[3:], jnp.bfloat16), pltpu.VMEM(work + flags[3:], jnp.int32),
+                dma((parts, depth)), dma((parts, depth)), dma((parts // 2, depth)), dma((parts // 2, depth)),
+                dma((depth,)), dma((depth,)), dma((depth,)), dma((depth,)),
+                dma((parts, depth)), dma((parts, depth)), dma((parts // 2, depth)), dma((parts // 2, depth)),
+                dma((parts,)), dma((parts,)), dma((parts // 2,)), dma((parts // 2,)),
+                dma((parts, 3)), dma((parts, 2)), dma((parts, 3)), dma((parts, 2)), dma((2,)),
+            ],
+            compiler_params=pltpu.CompilerParams(
+                collective_id=0, has_side_effects=True, vmem_limit_bytes=24 * 1024 * 1024
+            ),
+        )(*[pltpu.with_memory_space_constraint(x, pltpu.HBM) for x in (
+            flux_scale, patch_lists, visit_tiles.reshape(visits, own * rows, columns), warp_matrix,
+            clip_bits.reshape(entries, rows // 16, columns))])
+        return pl.pallas_call(
+            split, out_shape=(out, out), in_specs=[vmem], out_specs=(hbm, hbm),
+            scratch_shapes=[dma((2,))],
+            compiler_params=pltpu.CompilerParams(vmem_limit_bytes=8 * 1024 * 1024),
+        )(both)
     targets = patch_lists.reshape(entries)
     number = jnp.arange(entries, dtype=jnp.int32)
     same = (targets[:, None] == targets[None, :]) & (number[None, :] < number[:, None])
@@ -462,53 +591,6 @@
         jnp.where(slot[None, :] == jnp.arange(patches * CAPACITY, dtype=jnp.int32)[:, None], number[None, :], entries),
         axis=1,
     )
-    smem, vmem = pl.BlockSpec(memory_space=pltpu.SMEM), pl.BlockSpec(memory_space=pltpu.VMEM)
-    hbm = pl.BlockSpec(memory_space=pltpu.HBM)
-    out = jax.ShapeDtypeStruct((2, PATCH_DEV, share, columns), jnp.float32)
-    if sky == 4:
-        width = 128
-        slab = 8
-        parts = columns // width * (share // slab)
-        long = -(-patches * CAPACITY // 128) * 128
-        table = jnp.pad(source, (0, long - patches * CAPACITY), constant_values=entries)[None, :]
-        blocks = (parts, depth, entries, slab, width)
-        flags = (parts // 2, depth, entries, 1, width)
-        work = (2, depth, entries + 1)
-        dma = pltpu.SemaphoreType.DMA
-        both = pl.pallas_call(
-            functools.partial(folded, depth),
-            out_shape=jax.ShapeDtypeStruct((2,) + out.shape, jnp.float32),
-            in_specs=[smem, vmem, hbm, hbm, hbm],
-            out_specs=vmem,
-            scratch_shapes=[
-                pltpu.VMEM((visits, own * rows, columns), jnp.bfloat16),
-                pltpu.VMEM((columns // width, visits, columns, width), jnp.bfloat16),
-                pltpu.VMEM((entries, rows // 16, columns), jnp.int32),
-                dma((columns // width + 2,)),
-                pltpu.VMEM(blocks, jnp.bfloat16), pltpu.VMEM(flags, jnp.int32),
-                pltpu.VMEM(blocks, jnp.bfloat16), pltpu.VMEM(flags, jnp.int32), pltpu.VMEM((depth, 1, long), jnp.int32),
-                pltpu.VMEM(blocks, jnp.bfloat16), pltpu.VMEM(flags, jnp.int32), pltpu.VMEM((depth, 1, long), jnp.int32),
-                pltpu.VMEM((parts, 3, PATCH_DEV, 4, slab, width), jnp.float32),
-                pltpu.VMEM((parts, 3, PATCH_DEV, 2, slab, width), jnp.bfloat16),
-                pltpu.VMEM((parts, 2, PATCH_DEV, 4, slab, width), jnp.float32),
-                pltpu.VMEM((parts, 2, PATCH_DEV, 2, slab, width), jnp.bfloat16),
-                pltpu.SMEM((2, depth, 1, long), jnp.int32),
-                pltpu.VMEM((PATCH_DEV, 6, slab, width), jnp.float32),
-                pltpu.VMEM(work + blocks[3:], jnp.bfloat16), pltpu.VMEM(work + flags[3:], jnp.int32),
-                dma((parts, depth)), dma((parts, depth)), dma((parts // 2, depth)), dma((parts // 2, depth)),
-                dma((depth,)), dma((depth,)),
-                dma((parts,)), dma((parts,)), dma((parts // 2,)), dma((parts // 2,)), dma((1,)), dma((1,)),
-                dma((parts, 3)), dma((parts, 2)), dma((parts, 3)), dma((parts, 2)), dma((2,)),
-            ],
-            compiler_params=pltpu.CompilerParams(
-                collective_id=0, has_side_effects=True, vmem_limit_bytes=67043328 - 1048576
-            ),
-        )(flux_scale, table, visit_tiles.reshape(visits, own * rows, columns), warp_matrix,
-          clip_bits.reshape(entries, rows // 16, columns))
-        return pl.pallas_call(
-            split, out_shape=(out, out), in_specs=[vmem], out_specs=(vmem, vmem),
-            compiler_params=pltpu.CompilerParams(vmem_limit_bytes=67043328 - 1048576),
-        )(both)
     return pl.pallas_call(
         functools.partial(kernel, sky, depth),
         out_shape=(out, out),

time: 52.5 us -> 43.9 us (0.84)
  Pallas kernels: 50.1 us -> 43.1 us
  local copies, waits for them, and re-layouts: 1.28 us -> 0 us
    pallas_call x1, Pallas kernels: 48.2 us -> 42.3 us  [per_device(): pl.pallas_call(functools.partial(folded, depth), out_shape=jax.ShapeDtype...]
    pallas_call x1, Pallas kernels: 1.85 us -> 0.81 us  [per_device(): pl.pallas_call(split, out_shape=(out, out), in_specs=[vmem], out_specs=(h...]
    reshape x1 -> x0, local copies, waits for them, and re-layouts: 0.76 us -> none  [per_device(): targets = patch_lists.reshape(entries)]
where the time goes in v1:
time: 43.9 us; the launch traced here: 43.7 us
  Pallas kernels  43.1 us (98%)
  between operations  0.64 us (1%)
    pallas_call x1, Pallas kernels, per_device(): pl.pallas_call(functools.partial(folded, depth), out_shape=jax.ShapeDtype...  42.3 us

profile of v1, /device:TPU:0, one launch (start us, length us, event | category | flops | bytes accessed | tf_op | source)
XLA Modules:
  0.0 43.7 jit_solution(5169033585594765935)
XLA Ops:
  0.6 42.3 %shard_map.68.both_ref = f32[2,2,4,16,512]{4,3,2,1,0:T(8,128)S(1)} custom-call(f32[4]{0:T(128)} %scale_hbm.1, s32[4,4]{1,0:T(4,128)} %lists_hbm.1, bf16[4,256,512]{2,1,0:T(8,128)(2,1)} %bitcast.2, bf16[4,512,512]{2,1,0:T(8,128)(2,1)} %matrix_hbm.1, s32[16,4,512]{2,1,0:T(4,128)} %bitcast.3), custom_call_target="tpu_custom_call" | custom-call | tf_op jit(solution)/shard_map/pallas_call | solution.py:544
  42.9 0.8 %shard_map.69 = (f32[2,4,16,512]{3,2,1,0:T(8,128)}, f32[2,4,16,512]{3,2,1,0:T(8,128)}) custom-call(f32[2,2,4,16,512]{4,3,2,1,0:T(8,128)S(1)} %shard_map.68.both_ref), custom_call_target="tpu_custom_call" | custom-call | tf_op jit(solution)/shard_map/pallas_call | solution.py:580

commit v2 on v1

--- a/solution.py
+++ b/solution.py
@@ -151,10 +151,8 @@
 
 def folded(depth, scale_hbm, lists_hbm, tiles_hbm, matrix_hbm, bits_hbm, out_ref,
            scale_ref, lists_ref, tiles_ref, matrix_ref, bits_ref, s_in,
-           out_t, out_b, row_t, row_b, raw_t, raw_b, own_s, row_s, raw_s, far32, far16, got32, got16, tables, local,
-           work_t, work_b,
-           s_xt, r_xt, s_xb, r_xb, s_xs, r_xs, s_ms, r_ms, s_dt, r_dt, s_db, r_db, s_ft, r_ft, s_fb, r_fb,
-           s_f, r_f, s_h, r_h, s_l):
+           out_t, out_b, row_t, row_b, raw_t, raw_b, own_s, held_s, far32, far16, got32, got16, tables, local,
+           work_t, work_b, s_x, s_y, s_s, r_x, r_y, r_s, r_g, s_l):
     z, d = lax.axis_index("sky"), lax.axis_index("depth")
     half = z // 2
     rem = z - 2 * half
@@ -205,40 +203,65 @@
         return pltpu.make_async_remote_copy(src_ref=src, dst_ref=dst, send_sem=send, recv_sem=recv, device_id=to,
                                             device_id_type=MESH)
 
-    def to_row(c, there, slot):
-        to = {"depth": there}
-        return remote(out_t.at[c, there], row_t.at[c, slot], s_xt.at[c, there], r_xt.at[c, slot], to)
-
-    def flags_to_row(b, there, slot):
-        to = {"depth": there}
-        return remote(out_b.at[b, there], row_b.at[b, slot], s_xb.at[b, there], r_xb.at[b, slot], to)
-
-    def table_to_row(there, slot):
-        return remote(own_s, row_s.at[slot], s_xs.at[there], r_xs.at[slot], {"depth": there})
-
-    def table_to_mates(there, slot):
-        return remote(own_s, raw_s.at[slot], s_ms.at[there], r_ms.at[slot], {"sky": mate, "depth": there})
-
-    def direct(c, there, slot):
+    def to_row(c, there):
+        return remote(out_t.at[c, there], row_t.at[c, d], s_x.at[0], r_x.at[c], {"depth": there})
+
+    def flags_to_row(b, there):
+        return remote(out_b.at[b, there], row_b.at[b, d], s_x.at[1], r_x.at[2 * b], {"depth": there})
+
+    def table_to_row(there):
+        return remote(own_s, held_s.at[d], s_s.at[0], r_s.at[0], {"depth": there})
+
+    def table_to_mates(there):
+        return remote(own_s, held_s.at[depth + d], s_s.at[0], r_s.at[1], {"sky": mate, "depth": there})
+
+    def direct(c, there):
         to = {"sky": mate, "depth": there}
-        return remote(out_t.at[c, there], raw_t.at[c, slot], s_dt.at[c, there], r_dt.at[c, slot], to)
-
-    def flags_direct(b, there, slot):
+        return remote(out_t.at[c, there], raw_t.at[c, d], s_y.at[0], r_y.at[c], to)
+
+    def flags_direct(b, there):
         to = {"sky": mate, "depth": there}
-        return remote(out_b.at[b, there], raw_b.at[b, slot], s_db.at[b, there], r_db.at[b, slot], to)
-
-    def onward(c, start):
-        pair = pl.ds(start, 2)
-        return remote(row_t.at[c, pair], raw_t.at[c, pair], s_ft.at[c], r_ft.at[c], {"sky": mate})
-
-    def flags_onward(b, start):
-        pair = pl.ds(start, 2)
-        return remote(row_b.at[b, pair], raw_b.at[b, pair], s_fb.at[b], r_fb.at[b], {"sky": mate})
+        return remote(out_b.at[b, there], raw_b.at[b, d], s_y.at[1], r_y.at[2 * b], to)
+
+    def onward(c):
+        pair = pl.ds(other, 2)
+        return remote(row_t.at[c, pair], raw_t.at[c, pair], s_y.at[0], r_y.at[c], {"sky": mate})
+
+    def flags_onward(b):
+        pair = pl.ds(other, 2)
+        return remote(row_b.at[b, pair], raw_b.at[b, pair], s_y.at[1], r_y.at[2 * b], {"sky": mate})
 
     def sums_to(c, t, where, slot):
         to = {"sky": where}
-        return (remote(far32.at[c, t], got32.at[c, slot], s_f.at[c, t], r_f.at[c, slot], to),
-                remote(far16.at[c, t], got16.at[c, slot], s_h.at[c, t], r_h.at[c, slot], to))
+        return (remote(far32.at[c, t], got32.at[c, slot], s_y.at[0], r_g.at[c], to),
+                remote(far16.at[c, t], got16.at[c, slot], s_y.at[1], r_g.at[c], to))
+
+    def arrived(ref, sem):
+        remote(ref, ref, s_x.at[0], sem, {"sky": mate}).wait_recv()
+
+    def left(ref, sem):
+        remote(ref, ref, sem, r_s.at[0], {"sky": mate}).wait_send()
+
+    def row_arrived(c):
+        @pl.when(c % 2 == 0)
+        def _():
+            arrived(out_t.at[0, :, pl.ds(0, entries * 15 // 16)], r_x.at[c])
+
+        @pl.when(c % 2 == 1)
+        def _():
+            arrived(out_t.at[0, pl.ds(0, depth - 1)], r_x.at[c])
+
+    def raw_arrived(c):
+        @pl.when(c % 2 == 0)
+        def _():
+            arrived(out_t.at[pl.ds(0, depth + 1), 0], r_y.at[c])
+
+        @pl.when(c % 2 == 1)
+        def _():
+            arrived(out_t.at[0], r_y.at[c])
+
+    def sums_arrived(c, slots):
+        arrived(out_t.at[0, pl.ds(0, 2 * slots), pl.ds(0, PATCH_DEV * 7 // 2)], r_g.at[c])
 
     position = lax.broadcasted_iota(jnp.int32, (slab, width), 0)
     for which in range(2):
@@ -256,7 +279,7 @@
             rank = rank + (targets[e] == targets[f]).astype(jnp.int32)
         table = jnp.where(lane == targets[e] * CAPACITY + rank, e, table)
     own_s[...] = table
-    row_s[d] = table
+    held_s[d] = table
 
     def stage(c, which, tiles, flags):
         work_t[which, :, :entries] = tiles[c]
@@ -295,9 +318,9 @@
         @pl.when(c % 2 == 0)
         def _():
             for j in range(2):
-                flags_direct(c // 2, base + j, d).start()
+                flags_direct(c // 2, base + j).start()
         for j in range(2):
-            direct(c, base + j, d).start()
+            direct(c, base + j).start()
 
     def warp(column, _):
         lanes = pl.ds(pl.multiple_of(column * width, width), width)
@@ -330,19 +353,19 @@
             def _():
                 pl.semaphore_wait(barrier, 2 * depth)
             for k in range(1, depth):
-                table_to_row(lax.rem(d + k, depth), d).start()
+                table_to_row(lax.rem(d + k, depth)).start()
 
             @pl.when(outer)
             def _():
                 for k in range(depth):
-                    table_to_mates(k, d).start()
+                    table_to_mates(k).start()
 
         for h in range(slabs):
             for k in range(1, depth):
                 there = lax.rem(d + k, depth)
                 if h % 2 == 0:
-                    flags_to_row(column * groups_here + h // 2, there, d).start()
-                to_row(column * slabs + h, there, d).start()
+                    flags_to_row(column * groups_here + h // 2, there).start()
+                to_row(column * slabs + h, there).start()
 
             @pl.when(jnp.logical_and(outer, column * slabs + h < LEAD))
             def _(h=h):
@@ -355,9 +378,8 @@
     lax.fori_loop(0, bands, warp, 0)
     mine, theirs = (row_t, row_b), (raw_t, raw_b)
 
-    for k in range(1, depth):
-        table_to_row(lax.rem(d + k, depth), lax.rem(d + depth - k, depth)).wait_recv()
-    held = pltpu.make_async_copy(row_s, tables.at[0], s_l.at[0])
+    arrived(held_s.at[pl.ds(0, depth - 1)], r_s.at[0])
+    held = pltpu.make_async_copy(held_s.at[pl.ds(0, depth)], tables.at[0], s_l.at[0])
     held.start()
     held.wait()
 
@@ -382,6 +404,7 @@
                     local[p, q] = value
                 return 0
             lax.fori_loop(0, PATCH_DEV, one, 0)
+            sums_arrived(c, 1)
 
         @pl.when(outer)
         def _():
@@ -390,14 +413,11 @@
                     local[p, q] = value
                 return 0
             lax.fori_loop(0, PATCH_DEV, one, 0)
-            for copy in sums_to(c, 2, mate, half):
-                copy.wait_recv()
+            sums_arrived(c, 2)
             for p in range(PATCH_DEV):
                 for q, value in enumerate(total(c, half, p)):
                     local[p, q] = local[p, q] + value
 
-        for copy in sums_to(c, 0, across, 1 - half):
-            copy.wait_recv()
         for p in range(PATCH_DEV):
             cf, sf, qf, cb, sb, qb = [local[p, q] + value for q, value in enumerate(total(c, 1 - half, p))]
             mean = sf / jnp.maximum(cf, 1.0)
@@ -410,27 +430,18 @@
             out_ref[1, 1, p, lines, lanes] = (square - shift * step) / jnp.maximum(cb - 1.0, 1.0)
 
     def forward(c, _):
-        fresh = c % 2 == 0
-        b = c // 2
-
-        @pl.when(fresh)
-        def _():
-            for k in range(1, depth):
-                flags_to_row(b, lax.rem(d + k, depth), lax.rem(d + depth - k, depth)).wait_recv()
-
-        for k in range(1, depth):
-            to_row(c, lax.rem(d + k, depth), lax.rem(d + depth - k, depth)).wait_recv()
+        row_arrived(c)
 
         @pl.when(outer)
         def _():
-            @pl.when(fresh)
-            def _():
-                flags_onward(b, other).start()
-            onward(c, other).start()
-
-            @pl.when(c + LEAD < parts)
-            def _():
-                send_direct(c + LEAD)
+            @pl.when(c % 2 == 0)
+            def _():
+                flags_onward(c // 2).start()
+            onward(c).start()
+
+            @pl.when(jnp.logical_and(c >= 1, c + 1 < parts))
+            def _():
+                send_direct(c + 1)
 
         @pl.when(inner)
         def _():
@@ -439,21 +450,12 @@
 
             @pl.when(c == 0)
             def _():
-                for k in range(depth):
-                    table_to_mates(k, k).wait_recv()
-                more = pltpu.make_async_copy(raw_s, tables.at[1], s_l.at[1])
+                arrived(held_s.at[pl.ds(0, depth)], r_s.at[1])
+                more = pltpu.make_async_copy(held_s.at[pl.ds(depth, depth)], tables.at[1], s_l.at[1])
                 more.start()
                 more.wait()
 
-            @pl.when(fresh)
-            def _():
-                for j in range(2):
-                    flags_direct(b, base + j, base + j).wait_recv()
-                flags_onward(b, other).wait_recv()
-
-            for j in range(2):
-                direct(c, base + j, base + j).wait_recv()
-            onward(c, other).wait_recv()
+            raw_arrived(c)
             stage(c, 1, *theirs)
             send_sums(c, 0, beyond, 2)
             send_sums(c, 1, across, 2)
@@ -473,45 +475,20 @@
 
     lax.fori_loop(0, parts, close, 0)
 
-    for k in range(1, depth):
-        table_to_row(lax.rem(d + k, depth), d).wait_send()
+    left(out_t.at[:, pl.ds(0, depth - 1)], s_x.at[0])
+    left(out_b.at[:, pl.ds(0, depth - 1)], s_x.at[1])
 
     @pl.when(outer)
     def _():
-        for k in range(depth):
-            table_to_mates(k, d).wait_send()
-
-    def drain_flags(b, _):
-        for k in range(1, depth):
-            flags_to_row(b, lax.rem(d + k, depth), d).wait_send()
-
-        @pl.when(outer)
-        def _():
-            for j in range(2):
-                flags_direct(b, base + j, d).wait_send()
-            flags_onward(b, other).wait_send()
-        return 0
-
-    lax.fori_loop(0, parts // 2, drain_flags, 0)
-
-    def drain(c, _):
-        for k in range(1, depth):
-            to_row(c, lax.rem(d + k, depth), d).wait_send()
-
-        @pl.when(outer)
-        def _():
-            for j in range(2):
-                direct(c, base + j, d).wait_send()
-            onward(c, other).wait_send()
-
-        @pl.when(inner)
-        def _():
-            for t, where in ((0, beyond), (1, across), (2, mate)):
-                for copy in sums_to(c, t, where, half):
-                    copy.wait_send()
-        return 0
-
-    lax.fori_loop(0, parts, drain, 0)
+        left(held_s.at[pl.ds(0, 2 * depth - 1)], s_s.at[0])
+        left(out_t, s_y.at[0])
+        left(out_b, s_y.at[1])
+
+    @pl.when(inner)
+    def _():
+        left(held_s.at[pl.ds(0, depth - 1)], s_s.at[0])
+        left(far32, s_y.at[0])
+        left(far16, s_y.at[1])
 
 
 def split(both_ref, mean_hbm, var_hbm, sems):
@@ -556,8 +533,7 @@
                 pltpu.VMEM(blocks, jnp.bfloat16), pltpu.VMEM(flags, jnp.int32),
                 pltpu.VMEM(blocks, jnp.bfloat16), pltpu.VMEM(flags, jnp.int32),
                 pltpu.VMEM(blocks, jnp.bfloat16), pltpu.VMEM(flags, jnp.int32),
-                pltpu.VMEM((1, long), jnp.int32),
-                pltpu.VMEM((depth, 1, long), jnp.int32), pltpu.VMEM((depth, 1, long), jnp.int32),
+                pltpu.VMEM((1, long), jnp.int32), pltpu.VMEM((2 * depth, 1, long), jnp.int32),
                 pltpu.VMEM((parts, 3, PATCH_DEV, slab, width), jnp.float32),
                 pltpu.VMEM((parts, 3, PATCH_DEV, 5, slab, width), jnp.bfloat16),
                 pltpu.VMEM((parts, 2, PATCH_DEV, slab, width), jnp.float32),
@@ -565,11 +541,7 @@
                 pltpu.SMEM((2, depth, 1, long), jnp.int32),
                 pltpu.VMEM((PATCH_DEV, 6, slab, width), jnp.float32),
                 pltpu.VMEM(work + blocks[3:], jnp.bfloat16), pltpu.VMEM(work + flags[3:], jnp.int32),
-                dma((parts, depth)), dma((parts, depth)), dma((parts // 2, depth)), dma((parts // 2, depth)),
-                dma((depth,)), dma((depth,)), dma((depth,)), dma((depth,)),
-                dma((parts, depth)), dma((parts, depth)), dma((parts // 2, depth)), dma((parts // 2, depth)),
-                dma((parts,)), dma((parts,)), dma((parts // 2,)), dma((parts // 2,)),
-                dma((parts, 3)), dma((parts, 2)), dma((parts, 3)), dma((parts, 2)), dma((2,)),
+                dma((2,)), dma((2,)), dma((1,)), dma((parts,)), dma((parts,)), dma((2,)), dma((parts,)), dma((2,)),
             ],
             compiler_params=pltpu.CompilerParams(
                 collective_id=0, has_side_effects=True, vmem_limit_bytes=24 * 1024 * 1024

time: 43.9 us -> 40.1 us (0.913)
  Pallas kernels: 43.1 us -> 39.3 us
    pallas_call x1, Pallas kernels: 42.3 us -> 38.5 us  [per_device(): pl.pallas_call(functools.partial(folded, depth), out_shape=jax.ShapeDtype...]
where the time goes in v2:
time: 40.1 us; the launch traced here: 39.9 us
  Pallas kernels  39.3 us (98%)
  between operations  0.64 us (2%)
    pallas_call x1, Pallas kernels, per_device(): pl.pallas_call(functools.partial(folded, depth), out_shape=jax.ShapeDtype...  38.5 us
    pallas_call x1, Pallas kernels, per_device(): pl.pallas_call(split, out_shape=(out, out), in_specs=[vmem], out_specs=(h...  0.81 us

profile of v2, /device:TPU:0, one launch (start us, length us, event | category | flops | bytes accessed | tf_op | source)
XLA Modules:
  0.0 39.9 jit_solution(1545587738974139037)
XLA Ops:
  0.6 38.5 %shard_map.68.both_ref = f32[2,2,4,16,512]{4,3,2,1,0:T(8,128)S(1)} custom-call(f32[4]{0:T(128)} %scale_hbm.1, s32[4,4]{1,0:T(4,128)} %lists_hbm.1, bf16[4,256,512]{2,1,0:T(8,128)(2,1)} %bitcast.2, bf16[4,512,512]{2,1,0:T(8,128)(2,1)} %matrix_hbm.1, s32[16,4,512]{2,1,0:T(4,128)} %bitcast.3), custom_call_target="tpu_custom_call" | custom-call | tf_op jit(solution)/shard_map/pallas_call | solution.py:521
  39.1 0.8 %shard_map.69 = (f32[2,4,16,512]{3,2,1,0:T(8,128)}, f32[2,4,16,512]{3,2,1,0:T(8,128)}) custom-call(f32[2,2,4,16,512]{4,3,2,1,0:T(8,128)S(1)} %shard_map.68.both_ref), custom_call_target="tpu_custom_call" | custom-call | tf_op jit(solution)/shard_map/pallas_call | solution.py:552

commit v3 on v2

--- a/solution.py
+++ b/solution.py
@@ -12,8 +12,11 @@
 SLOTS = PATCH_DEV * CAPACITY
 MESH = pl.DeviceIdType.MESH
 STEP = 4
-LAG = 3
-LEAD = 2
+LAG = 5
+LEAD = 5
+SLAB = 4
+SWAP = 2
+TURN = 5
 
 
 def kernel(sky, depth, scale_ref, src_ref, tiles_ref, matrix_ref, bits_ref, mean_ref, var_ref,
@@ -161,8 +164,8 @@
     across, beyond = 3 - z, 3 - mate
     base = d // 2 * 2
     other = depth - 2 - base
+    twin = 2 * base + 1 - d
     parts, _, entries, slab, width = out_t.shape
-    groups_here = out_b.shape[0] * width // tiles_ref.shape[2]
     visits, entries_rows, columns = tiles_ref.shape
     per_visit = entries // visits
     rows = entries_rows // per_visit
@@ -171,6 +174,18 @@
     long = own_s.shape[1]
 
     bands = matrix_ref.shape[0]
+    first = bands // 2 * slabs - SWAP
+    chain = parts - SWAP
+
+    def chunk(i):
+        return i + jnp.where(i >= first, SWAP, 0)
+
+    def swapped(c):
+        return jnp.logical_and(c >= first, c < first + SWAP)
+
+    def fresh(c):
+        return jnp.logical_or(c % slabs == 0, c == first)
+
     tiles_in = pltpu.make_async_copy(tiles_hbm, tiles_ref, s_in.at[bands])
     bits_in = pltpu.make_async_copy(bits_hbm, bits_ref, s_in.at[bands + 1])
     scale_in = pltpu.make_async_copy(scale_hbm, scale_ref, s_in.at[bands + 2])
@@ -185,11 +200,8 @@
         pl.semaphore_signal(barrier, inc=1, device_id={"depth": lax.rem(d + k, depth)}, device_id_type=MESH)
     for k in range(depth):
         pl.semaphore_signal(barrier, inc=1, device_id={"sky": mate, "depth": k}, device_id_type=MESH)
-    pl.semaphore_signal(barrier, inc=1, device_id={"sky": beyond}, device_id_type=MESH)
-
-    @pl.when(inner)
-    def _():
-        pl.semaphore_signal(barrier, inc=1, device_id={"sky": across}, device_id_type=MESH)
+    for far in (across, beyond):
+        pl.semaphore_signal(barrier, inc=1, device_id={"sky": far}, device_id_type=MESH)
 
     tiles_in.start()
     matrix_in(0).start()
@@ -207,7 +219,7 @@
         return remote(out_t.at[c, there], row_t.at[c, d], s_x.at[0], r_x.at[c], {"depth": there})
 
     def flags_to_row(b, there):
-        return remote(out_b.at[b, there], row_b.at[b, d], s_x.at[1], r_x.at[2 * b], {"depth": there})
+        return remote(out_b.at[b, there], row_b.at[b, d], s_x.at[1], r_x.at[slabs * b], {"depth": there})
 
     def table_to_row(there):
         return remote(own_s, held_s.at[d], s_s.at[0], r_s.at[0], {"depth": there})
@@ -219,22 +231,23 @@
         to = {"sky": mate, "depth": there}
         return remote(out_t.at[c, there], raw_t.at[c, d], s_y.at[0], r_y.at[c], to)
 
-    def flags_direct(b, there):
+    def flags_direct(c, there):
         to = {"sky": mate, "depth": there}
-        return remote(out_b.at[b, there], raw_b.at[b, d], s_y.at[1], r_y.at[2 * b], to)
+        b = c // slabs
+        return remote(out_b.at[b, there], raw_b.at[b, d], s_y.at[1], r_y.at[c], to)
 
     def onward(c):
         pair = pl.ds(other, 2)
         return remote(row_t.at[c, pair], raw_t.at[c, pair], s_y.at[0], r_y.at[c], {"sky": mate})
 
-    def flags_onward(b):
-        pair = pl.ds(other, 2)
-        return remote(row_b.at[b, pair], raw_b.at[b, pair], s_y.at[1], r_y.at[2 * b], {"sky": mate})
+    def flags_onward(c):
+        b, pair = c // slabs, pl.ds(other, 2)
+        return remote(row_b.at[b, pair], raw_b.at[b, pair], s_y.at[1], r_y.at[c], {"sky": mate})
 
     def sums_to(c, t, where, slot):
         to = {"sky": where}
-        return (remote(far32.at[c, t], got32.at[c, slot], s_y.at[0], r_g.at[c], to),
-                remote(far16.at[c, t], got16.at[c, slot], s_y.at[1], r_g.at[c], to))
+        return (remote(far32.at[c, t], got32.at[c, slot], s_y.at[2], r_g.at[c], to),
+                remote(far16.at[c, t], got16.at[c, slot], s_y.at[3], r_g.at[c], to))
 
     def arrived(ref, sem):
         remote(ref, ref, s_x.at[0], sem, {"sky": mate}).wait_recv()
@@ -242,26 +255,30 @@
     def left(ref, sem):
         remote(ref, ref, sem, r_s.at[0], {"sky": mate}).wait_send()
 
+    def volume(tiles):
+        a, b, k = next((a, b, k) for a in range(1, parts + 1) for b in range(1, depth + 1)
+                       for k in range(1, entries + 1) if a * b * k == tiles)
+        return out_t.at[pl.ds(0, a), pl.ds(0, b), pl.ds(0, k)]
+
+    def blocks_arrived(c, flags, sem, count):
+        flag_tiles = 2 * entries // slab
+
+        @pl.when(flags)
+        def _():
+            arrived(volume(count * (entries + flag_tiles)), sem.at[c])
+
+        @pl.when(jnp.logical_not(flags))
+        def _():
+            arrived(volume(count * entries), sem.at[c])
+
     def row_arrived(c):
-        @pl.when(c % 2 == 0)
-        def _():
-            arrived(out_t.at[0, :, pl.ds(0, entries * 15 // 16)], r_x.at[c])
-
-        @pl.when(c % 2 == 1)
-        def _():
-            arrived(out_t.at[0, pl.ds(0, depth - 1)], r_x.at[c])
+        blocks_arrived(c, c % slabs == 0, r_x, depth - 1)
 
     def raw_arrived(c):
-        @pl.when(c % 2 == 0)
-        def _():
-            arrived(out_t.at[pl.ds(0, depth + 1), 0], r_y.at[c])
-
-        @pl.when(c % 2 == 1)
-        def _():
-            arrived(out_t.at[0], r_y.at[c])
+        blocks_arrived(c, fresh(c), r_y, depth)
 
     def sums_arrived(c, slots):
-        arrived(out_t.at[0, pl.ds(0, 2 * slots), pl.ds(0, PATCH_DEV * 7 // 2)], r_g.at[c])
+        arrived(volume(slots * PATCH_DEV * 7), r_g.at[c])
 
     position = lax.broadcasted_iota(jnp.int32, (slab, width), 0)
     for which in range(2):
@@ -283,10 +300,10 @@
 
     def stage(c, which, tiles, flags):
         work_t[which, :, :entries] = tiles[c]
-        work_b[which, :, :entries] = flags[c // 2]
+        work_b[which, :, :entries] = flags[c // slabs]
 
     def gather(c, patch, groups):
-        place = position + (c % 2) * slab
+        place = position + (c % slabs) * slab
         sums = [jnp.zeros((slab, width), jnp.float32)] * 6
         for which in range(groups):
             for dd in range(depth):
@@ -315,12 +332,18 @@
             copy.start()
 
     def send_direct(c):
-        @pl.when(c % 2 == 0)
+        @pl.when(fresh(c))
         def _():
             for j in range(2):
-                flags_direct(c // 2, base + j).start()
+                flags_direct(c, base + j).start()
         for j in range(2):
             direct(c, base + j).start()
+
+    def send_onward(c):
+        @pl.when(fresh(c))
+        def _():
+            flags_onward(c).start()
+        onward(c).start()
 
     def warp(column, _):
         lanes = pl.ds(pl.multiple_of(column * width, width), width)
@@ -334,42 +357,35 @@
             for dd in range(depth):
                 for h in range(slabs):
                     out_t[column * slabs + h, dd, v * per_visit:(v + 1) * per_visit] = block[:, dd, h].astype(jnp.bfloat16)
-        for g in range(groups_here):
-            b = column * groups_here + g
-            for dd in range(depth):
-                line = dd * groups_here + g
-                out_b[b, dd] = bits_ref[:, line:line + 1, lanes]
-            row_b[b, d] = out_b[b, d]
+        for dd in range(depth):
+            out_b[column, dd] = bits_ref[:, dd:dd + 1, lanes]
+        row_b[column, d] = out_b[column, d]
         for h in range(slabs):
             row_t[column * slabs + h, d] = out_t[column * slabs + h, d]
 
         @pl.when(column == 0)
         def _():
-            @pl.when(inner)
-            def _():
-                pl.semaphore_wait(barrier, 2 * depth + 1)
-
-            @pl.when(outer)
-            def _():
-                pl.semaphore_wait(barrier, 2 * depth)
-            for k in range(1, depth):
-                table_to_row(lax.rem(d + k, depth)).start()
-
-            @pl.when(outer)
-            def _():
-                for k in range(depth):
-                    table_to_mates(k).start()
+            pl.semaphore_wait(barrier, 2 * depth + 1)
 
         for h in range(slabs):
-            for k in range(1, depth):
-                there = lax.rem(d + k, depth)
-                if h % 2 == 0:
-                    flags_to_row(column * groups_here + h // 2, there).start()
+            for there in (other, other + 1, twin):
+                if h == 0:
+                    flags_to_row(column, there).start()
                 to_row(column * slabs + h, there).start()
 
-            @pl.when(jnp.logical_and(outer, column * slabs + h < LEAD))
-            def _(h=h):
-                send_direct(column * slabs + h)
+            c = column * slabs + h
+
+            @pl.when(jnp.logical_or(jnp.logical_and(outer, c < LEAD), jnp.logical_and(inner, swapped(c))))
+            def _(c=c):
+                send_direct(c)
+
+            if h == 0:
+                @pl.when(column == 0)
+                def _():
+                    for k in range(1, depth):
+                        table_to_row(lax.rem(d + k, depth)).start()
+                    for k in range(depth):
+                        table_to_mates(k).start()
         return 0
 
     tiles_in.wait()
@@ -378,10 +394,11 @@
     lax.fori_loop(0, bands, warp, 0)
     mine, theirs = (row_t, row_b), (raw_t, raw_b)
 
-    arrived(held_s.at[pl.ds(0, depth - 1)], r_s.at[0])
-    held = pltpu.make_async_copy(held_s.at[pl.ds(0, depth)], tables.at[0], s_l.at[0])
-    held.start()
-    held.wait()
+    def row_tables():
+        arrived(held_s.at[pl.ds(0, depth - 1)], r_s.at[0])
+        held = pltpu.make_async_copy(held_s.at[pl.ds(0, depth)], tables.at[0], s_l.at[0])
+        held.start()
+        held.wait()
 
     def total(c, slot, p):
         sf = got32[c, slot, p]
@@ -390,87 +407,125 @@
         sb = shift + mean * cb
         return cf, sf, mf + sf * mean, cb, sb, mb + sb * (sb / jnp.maximum(cb, 1.0))
 
+    def keep_local(c, groups):
+        def one(p, _):
+            for q, value in enumerate(gather(c, z * PATCH_DEV + p, groups)):
+                local[c, p, q] = value
+            return 0
+        lax.fori_loop(0, PATCH_DEV, one, 0)
+
     def finish(c):
         lanes = pl.ds(pl.multiple_of(c // slabs * width, width), width)
-        lines = pl.ds(pl.multiple_of(c % slabs * slab, slab), slab)
-        stage(c, 0, *mine)
-
-        @pl.when(inner)
-        def _():
-            stage(c, 1, *theirs)
-
-            def one(p, _):
-                for q, value in enumerate(gather(c, z * PATCH_DEV + p, 2)):
-                    local[p, q] = value
-                return 0
-            lax.fori_loop(0, PATCH_DEV, one, 0)
+        hub = jnp.logical_xor(inner, swapped(c))
+
+        @pl.when(hub)
+        def _():
             sums_arrived(c, 1)
 
-        @pl.when(outer)
-        def _():
-            def one(p, _):
-                for q, value in enumerate(gather(c, z * PATCH_DEV + p, 1)):
-                    local[p, q] = value
-                return 0
-            lax.fori_loop(0, PATCH_DEV, one, 0)
+        @pl.when(jnp.logical_not(hub))
+        def _():
             sums_arrived(c, 2)
             for p in range(PATCH_DEV):
                 for q, value in enumerate(total(c, half, p)):
-                    local[p, q] = local[p, q] + value
+                    local[c, p, q] = local[c, p, q] + value
 
         for p in range(PATCH_DEV):
-            cf, sf, qf, cb, sb, qb = [local[p, q] + value for q, value in enumerate(total(c, 1 - half, p))]
+            cf, sf, qf, cb, sb, qb = [local[c, p, q] + value for q, value in enumerate(total(c, 1 - half, p))]
             mean = sf / jnp.maximum(cf, 1.0)
             shift = sb - mean * cb
             square = qb - mean * sb - mean * shift
             step = shift / jnp.maximum(cb, 1.0)
-            out_ref[0, 0, p, lines, lanes] = mean
-            out_ref[0, 1, p, lines, lanes] = mean + step
-            out_ref[1, 0, p, lines, lanes] = (qf - sf * mean) / jnp.maximum(cf - 1.0, 1.0)
-            out_ref[1, 1, p, lines, lanes] = (square - shift * step) / jnp.maximum(cb - 1.0, 1.0)
-
-    def forward(c, _):
-        row_arrived(c)
-
-        @pl.when(outer)
-        def _():
-            @pl.when(c % 2 == 0)
+            first_var = (qf - sf * mean) / jnp.maximum(cf - 1.0, 1.0)
+            final_var = (square - shift * step) / jnp.maximum(cb - 1.0, 1.0)
+            for h in range(slabs):
+                @pl.when(c % slabs == h)
+                def _(h=h, p=p, values=(mean, mean + step, first_var, final_var)):
+                    for q, value in enumerate(values):
+                        out_ref[q // 2, q % 2, p, h * slab:(h + 1) * slab, lanes] = value
+
+    def other_tables():
+        arrived(held_s.at[pl.ds(0, depth)], r_s.at[1])
+        more = pltpu.make_async_copy(held_s.at[pl.ds(depth, depth)], tables.at[1], s_l.at[1])
+        more.start()
+        more.wait()
+
+    @pl.when(outer)
+    def _():
+        def leaf(i, _):
+            c = chunk(i)
+            row_arrived(c)
+            send_onward(c)
+
+            @pl.when(jnp.logical_and(i >= LEAD - 1, i + 1 < chain))
             def _():
-                flags_onward(c // 2).start()
-            onward(c).start()
-
-            @pl.when(jnp.logical_and(c >= 1, c + 1 < parts))
+                send_direct(chunk(i + 1))
+            return 0
+
+        lax.fori_loop(0, chain, leaf, 0)
+        row_tables()
+        other_tables()
+
+        def own(i, _):
+            c = chunk(i)
+            stage(c, 0, *mine)
+            keep_local(c, 1)
+            return 0
+
+        lax.fori_loop(0, chain, own, 0)
+
+        def turned(c, _):
+            row_arrived(c)
+            raw_arrived(c)
+            stage(c, 0, *mine)
+            stage(c, 1, *theirs)
+            send_sums(c, 1, across, 2)
+            send_sums(c, 0, beyond, 2)
+            send_sums(c, 2, mate, 1)
+            keep_local(c, 2)
+            return 0
+
+        lax.fori_loop(first, first + SWAP, turned, 0)
+
+    @pl.when(inner)
+    def _():
+        row_tables()
+        other_tables()
+
+        def hub(i, _):
+            c = chunk(i)
+
+            row_arrived(c)
+
+            @pl.when(i == TURN)
             def _():
-                send_direct(c + 1)
-
-        @pl.when(inner)
-        def _():
+                def turned(q, _):
+                    row_arrived(q)
+                    send_onward(q)
+                    stage(q, 0, *mine)
+                    keep_local(q, 1)
+                    return 0
+                lax.fori_loop(first, first + SWAP, turned, 0)
+
             stage(c, 0, *mine)
             send_sums(c, 2, mate, 1)
-
-            @pl.when(c == 0)
-            def _():
-                arrived(held_s.at[pl.ds(0, depth)], r_s.at[1])
-                more = pltpu.make_async_copy(held_s.at[pl.ds(depth, depth)], tables.at[1], s_l.at[1])
-                more.start()
-                more.wait()
-
             raw_arrived(c)
             stage(c, 1, *theirs)
             send_sums(c, 0, beyond, 2)
             send_sums(c, 1, across, 2)
-
-            @pl.when(c >= LAG)
+            keep_local(c, 2)
+
+            @pl.when(i >= LAG)
             def _():
-                finish(c - LAG)
-        return 0
-
-    lax.fori_loop(0, parts, forward, 0)
-
-    def close(c, _):
-        @pl.when(jnp.logical_or(outer, c >= parts - LAG))
-        def _():
-            finish(c)
+                finish(chunk(i - LAG))
+            return 0
+
+        lax.fori_loop(0, chain, hub, 0)
+
+    def close(i, _):
+        @pl.when(jnp.logical_or(outer, i >= chain - LAG))
+        def _():
+            turn = jnp.logical_and(i >= chain - 1, i < parts - 1)
+            finish(jnp.where(turn, i - chain + 1 + first, chunk(jnp.minimum(i, chain - 1))))
         return 0
 
     lax.fori_loop(0, parts, close, 0)
@@ -478,17 +533,21 @@
     left(out_t.at[:, pl.ds(0, depth - 1)], s_x.at[0])
     left(out_b.at[:, pl.ds(0, depth - 1)], s_x.at[1])
 
+    left(held_s.at[pl.ds(0, 2 * depth - 1)], s_s.at[0])
+
+    def all_left(sent, bands_sent, summed):
+        left(out_t.at[pl.ds(0, sent)], s_y.at[0])
+        left(out_b.at[pl.ds(0, bands_sent)], s_y.at[1])
+        left(far32.at[pl.ds(0, summed)], s_y.at[2])
+        left(far16.at[pl.ds(0, summed)], s_y.at[3])
+
     @pl.when(outer)
     def _():
-        left(held_s.at[pl.ds(0, 2 * depth - 1)], s_s.at[0])
-        left(out_t, s_y.at[0])
-        left(out_b, s_y.at[1])
+        all_left(chain, bands, SWAP)
 
     @pl.when(inner)
     def _():
-        left(held_s.at[pl.ds(0, depth - 1)], s_s.at[0])
-        left(far32, s_y.at[0])
-        left(far16, s_y.at[1])
+        all_left(SWAP, 1, chain)
 
 
 def split(both_ref, mean_hbm, var_hbm, sems):
@@ -508,14 +567,14 @@
     smem, vmem = pl.BlockSpec(memory_space=pltpu.SMEM), pl.BlockSpec(memory_space=pltpu.VMEM)
     hbm = pl.BlockSpec(memory_space=pltpu.HBM)
     out = jax.ShapeDtypeStruct((2, PATCH_DEV, share, columns), jnp.float32)
-    if sky == 4 and depth == 4:
+    if sky == 4 and depth == 4 and share == 16:
         width = 128
-        slab = 8
+        slab = SLAB
         bands = columns // width
         parts = bands * (share // slab)
         long = -(-patches * CAPACITY // 128) * 128
         blocks = (parts, depth, entries, slab, width)
-        flags = (parts // 2, depth, entries, 1, width)
+        flags = (bands, depth, entries, 1, width)
         work = (2, depth, entries + 1)
         dma = pltpu.SemaphoreType.DMA
         both = pl.pallas_call(
@@ -539,9 +598,9 @@
                 pltpu.VMEM((parts, 2, PATCH_DEV, slab, width), jnp.float32),
                 pltpu.VMEM((parts, 2, PATCH_DEV, 5, slab, width), jnp.bfloat16),
                 pltpu.SMEM((2, depth, 1, long), jnp.int32),
-                pltpu.VMEM((PATCH_DEV, 6, slab, width), jnp.float32),
+                pltpu.VMEM((parts, PATCH_DEV, 6, slab, width), jnp.float32),
                 pltpu.VMEM(work + blocks[3:], jnp.bfloat16), pltpu.VMEM(work + flags[3:], jnp.int32),
-                dma((2,)), dma((2,)), dma((1,)), dma((parts,)), dma((parts,)), dma((2,)), dma((parts,)), dma((2,)),
+                dma((2,)), dma((4,)), dma((1,)), dma((parts,)), dma((parts,)), dma((2,)), dma((parts,)), dma((2,)),
             ],
             compiler_params=pltpu.CompilerParams(
                 collective_id=0, has_side_effects=True, vmem_limit_bytes=24 * 1024 * 1024

time: 40.1 us -> 37.3 us (0.930)
  Pallas kernels: 39.3 us -> 36.5 us
    pallas_call x1, Pallas kernels: 38.5 us -> 35.7 us  [per_device(): pl.pallas_call(functools.partial(folded, depth), out_shape=jax.ShapeDtype...]
where the time goes in v3:
time: 37.3 us; the launch traced here: 37.1 us
  Pallas kernels  36.5 us (98%)
  between operations  0.64 us (2%)
    pallas_call x1, Pallas kernels, per_device(): pl.pallas_call(functools.partial(folded, depth), out_shape=jax.ShapeDtype...  35.7 us
    pallas_call x1, Pallas kernels, per_device(): pl.pallas_call(split, out_shape=(out, out), in_specs=[vmem], out_specs=(h...  0.81 us

profile of v3, /device:TPU:0, one launch (start us, length us, event | category | flops | bytes accessed | tf_op | source)
XLA Modules:
  0.0 37.1 jit_solution(11593405728561710478)
XLA Ops:
  0.6 35.7 %shard_map.68.both_ref = f32[2,2,4,16,512]{4,3,2,1,0:T(8,128)S(1)} custom-call(f32[4]{0:T(128)} %scale_hbm.1, s32[4,4]{1,0:T(4,128)} %lists_hbm.1, bf16[4,256,512]{2,1,0:T(8,128)(2,1)} %bitcast.2, bf16[4,512,512]{2,1,0:T(8,128)(2,1)} %matrix_hbm.1, s32[16,4,512]{2,1,0:T(4,128)} %bitcast.3), custom_call_target="tpu_custom_call" | custom-call | tf_op jit(solution)/shard_map/pallas_call | solution.py:580
  36.3 0.8 %shard_map.69 = (f32[2,4,16,512]{3,2,1,0:T(8,128)}, f32[2,4,16,512]{3,2,1,0:T(8,128)}) custom-call(f32[2,2,4,16,512]{4,3,2,1,0:T(8,128)S(1)} %shard_map.68.both_ref), custom_call_target="tpu_custom_call" | custom-call | tf_op jit(solution)/shard_map/pallas_call | solution.py:611

commit v4 on v3

--- a/solution.py
+++ b/solution.py
@@ -14,9 +14,11 @@
 STEP = 4
 LAG = 5
 LEAD = 5
+PRE = 5
 SLAB = 4
-SWAP = 2
-TURN = 5
+PIECES = 8
+SWAP = 3
+TURN = 8
 
 
 def kernel(sky, depth, scale_ref, src_ref, tiles_ref, matrix_ref, bits_ref, mean_ref, var_ref,
@@ -154,7 +156,7 @@
 
 def folded(depth, scale_hbm, lists_hbm, tiles_hbm, matrix_hbm, bits_hbm, out_ref,
            scale_ref, lists_ref, tiles_ref, matrix_ref, bits_ref, s_in,
-           out_t, out_b, row_t, row_b, raw_t, raw_b, own_s, held_s, far32, far16, got32, got16, tables, local,
+           out_t, out_b, row_t, row_b, raw_t, raw_b, own_s, held_s, far32, far16, got32, got16, tables, local, part,
            work_t, work_b, s_x, s_y, s_s, r_x, r_y, r_s, r_g, s_l):
     z, d = lax.axis_index("sky"), lax.axis_index("depth")
     half = z // 2
@@ -174,7 +176,7 @@
     long = own_s.shape[1]
 
     bands = matrix_ref.shape[0]
-    first = bands // 2 * slabs - SWAP
+    first = bands // 2 * slabs + slabs - SWAP
     chain = parts - SWAP
 
     def chunk(i):
@@ -208,8 +210,6 @@
     lists_in.start()
     scale_in.start()
     bits_in.start()
-    for band in range(1, bands):
-        matrix_in(band).start()
 
     def remote(src, dst, send, recv, to):
         return pltpu.make_async_remote_copy(src_ref=src, dst_ref=dst, send_sem=send, recv_sem=recv, device_id=to,
@@ -287,6 +287,8 @@
             work_b[which, dd, entries] = jnp.zeros((1, width), jnp.int32)
 
     lists_in.wait()
+    for band in range(1, bands):
+        matrix_in(band).start()
     lane = lax.broadcasted_iota(jnp.int32, (1, long), 1)
     table = jnp.full((1, long), entries, jnp.int32)
     targets = [lists_ref[v, k] for v in range(visits) for k in range(per_visit)]
@@ -302,10 +304,10 @@
         work_t[which, :, :entries] = tiles[c]
         work_b[which, :, :entries] = flags[c // slabs]
 
-    def gather(c, patch, groups):
+    def gather(c, patch, groups, start=0):
         place = position + (c % slabs) * slab
         sums = [jnp.zeros((slab, width), jnp.float32)] * 6
-        for which in range(groups):
+        for which in range(start, groups):
             for dd in range(depth):
                 for k in range(CAPACITY):
                     e = tables[which, dd, 0, patch * CAPACITY + k]
@@ -318,9 +320,19 @@
                     sums = [a + b for a, b in zip(sums, (first, fw, fw * w, both, bw, bw * w))]
         return sums
 
+    def keep_part(c, t, where):
+        def one(p, _):
+            for q, value in enumerate(gather(c, where * PATCH_DEV + p, 1)):
+                part[t, p, q] = value
+            return 0
+        lax.fori_loop(0, PATCH_DEV, one, 0)
+
     def send_sums(c, t, where, groups):
         def one(p, _):
-            cf, sf, qf, cb, sb, qb = gather(c, where * PATCH_DEV + p, groups)
+            sums = gather(c, where * PATCH_DEV + p, groups, groups - 1)
+            if groups == 2:
+                sums = [part[t, p, q] + value for q, value in enumerate(sums)]
+            cf, sf, qf, cb, sb, qb = sums
             mean = sf / jnp.maximum(cf, 1.0)
             far32[c, t, p] = sf
             packed = (cf, cb, qf - sf * mean, sb - mean * cb, qb - sb * (sb / jnp.maximum(cb, 1.0)))
@@ -375,7 +387,7 @@
 
             c = column * slabs + h
 
-            @pl.when(jnp.logical_or(jnp.logical_and(outer, c < LEAD), jnp.logical_and(inner, swapped(c))))
+            @pl.when(jnp.logical_or(jnp.logical_and(outer, c < PRE), jnp.logical_and(inner, swapped(c))))
             def _(c=c):
                 send_direct(c)
 
@@ -456,6 +468,10 @@
             row_arrived(c)
             send_onward(c)
 
+            @pl.when(i < LEAD - PRE)
+            def _():
+                send_direct(chunk(i + PRE))
+
             @pl.when(jnp.logical_and(i >= LEAD - 1, i + 1 < chain))
             def _():
                 send_direct(chunk(i + 1))
@@ -477,6 +493,8 @@
             row_arrived(c)
             raw_arrived(c)
             stage(c, 0, *mine)
+            keep_part(c, 0, beyond)
+            keep_part(c, 1, across)
             stage(c, 1, *theirs)
             send_sums(c, 1, across, 2)
             send_sums(c, 0, beyond, 2)
@@ -508,6 +526,8 @@
 
             stage(c, 0, *mine)
             send_sums(c, 2, mate, 1)
+            keep_part(c, 0, beyond)
+            keep_part(c, 1, across)
             raw_arrived(c)
             stage(c, 1, *theirs)
             send_sums(c, 0, beyond, 2)
@@ -551,11 +571,17 @@
 
 
 def split(both_ref, mean_hbm, var_hbm, sems):
-    copies = [pltpu.make_async_copy(both_ref.at[q], out, sems.at[q]) for q, out in enumerate((mean_hbm, var_hbm))]
-    for copy in copies:
-        copy.start()
-    for copy in copies:
-        copy.wait()
+    outs = (mean_hbm, var_hbm)
+    steps, patches = mean_hbm.shape[:2]
+    pieces = PIECES // steps
+    each = patches // pieces
+    for t in range(steps):
+        for p in range(pieces):
+            part = pl.ds(p * each, each)
+            for q, out in enumerate(outs):
+                pltpu.make_async_copy(both_ref.at[q, t, part], out.at[t, part], sems.at[q]).start()
+    for q, out in enumerate(outs):
+        pltpu.make_async_copy(both_ref.at[q], out, sems.at[q]).wait()
 
 
 def per_device(sky, depth, visit_tiles, warp_matrix, flux_scale, patch_lists, clip_bits):
@@ -599,6 +625,7 @@
                 pltpu.VMEM((parts, 2, PATCH_DEV, 5, slab, width), jnp.bfloat16),
                 pltpu.SMEM((2, depth, 1, long), jnp.int32),
                 pltpu.VMEM((parts, PATCH_DEV, 6, slab, width), jnp.float32),
+                pltpu.VMEM((2, PATCH_DEV, 6, slab, width), jnp.float32),
                 pltpu.VMEM(work + blocks[3:], jnp.bfloat16), pltpu.VMEM(work + flags[3:], jnp.int32),
                 dma((2,)), dma((4,)), dma((1,)), dma((parts,)), dma((parts,)), dma((2,)), dma((parts,)), dma((2,)),
             ],

time: 37.3 us -> 37.1 us (level)
  no operation moved by 1% of the time
where the time goes in v4:
time: 37.1 us; the launch traced here: 36.9 us
  Pallas kernels  36.3 us (98%)
  between operations  0.64 us (2%)
    pallas_call x1, Pallas kernels, per_device(): pl.pallas_call(functools.partial(folded, depth), out_shape=jax.ShapeDtype...  35.5 us
    pallas_call x1, Pallas kernels, per_device(): pl.pallas_call(split, out_shape=(out, out), in_specs=[vmem], out_specs=(h...  0.79 us

profile of v4, /device:TPU:0, one launch (start us, length us, event | category | flops | bytes accessed | tf_op | source)
XLA Modules:
  0.0 36.9 jit_solution(7882704451127988330)
XLA Ops:
  0.6 35.5 %shard_map.68.both_ref = f32[2,2,4,16,512]{4,3,2,1,0:T(8,128)S(1)} custom-call(f32[4]{0:T(128)} %scale_hbm.1, s32[4,4]{1,0:T(4,128)} %lists_hbm.1, bf16[4,256,512]{2,1,0:T(8,128)(2,1)} %bitcast.2, bf16[4,512,512]{2,1,0:T(8,128)(2,1)} %matrix_hbm.1, s32[16,4,512]{2,1,0:T(4,128)} %bitcast.3), custom_call_target="tpu_custom_call" | custom-call | tf_op jit(solution)/shard_map/pallas_call | solution.py:606
  36.2 0.8 %shard_map.69 = (f32[2,4,16,512]{3,2,1,0:T(8,128)}, f32[2,4,16,512]{3,2,1,0:T(8,128)}) custom-call(f32[2,2,4,16,512]{4,3,2,1,0:T(8,128)S(1)} %shard_map.68.both_ref), custom_call_target="tpu_custom_call" | custom-call | tf_op jit(solution)/shard_map/pallas_call | solution.py:638

commit v5 on v4

--- a/solution.py
+++ b/solution.py
@@ -343,6 +343,11 @@
         for copy in sums_to(c, t, where, half):
             copy.start()
 
+    def send_all(c):
+        for there in (other, other + 1, base, base + 1):
+            flags_direct(c, there).start()
+            direct(c, there).start()
+
     def send_direct(c):
         @pl.when(fresh(c))
         def _():
@@ -378,26 +383,40 @@
         @pl.when(column == 0)
         def _():
             pl.semaphore_wait(barrier, 2 * depth + 1)
-
-        for h in range(slabs):
+            for k in range(1, depth):
+                table_to_row(lax.rem(d + k, depth)).start()
+            for k in range(depth):
+                table_to_mates(k).start()
+
+        late = jnp.logical_and(outer, column == 0)
+
+        @pl.when(late)
+        def _():
+            send_all(0)
+
+        def spread(h):
             for there in (other, other + 1, twin):
                 if h == 0:
                     flags_to_row(column, there).start()
                 to_row(column * slabs + h, there).start()
 
+        for h in range(slabs):
             c = column * slabs + h
-
-            @pl.when(jnp.logical_or(jnp.logical_and(outer, c < PRE), jnp.logical_and(inner, swapped(c))))
+            if h == 0:
+                @pl.when(jnp.logical_not(late))
+                def _():
+                    spread(0)
+            else:
+                spread(h)
+            ahead = jnp.logical_and(outer, jnp.logical_and(c > 0, c < PRE))
+
+            @pl.when(jnp.logical_or(ahead, jnp.logical_and(inner, swapped(c))))
             def _(c=c):
                 send_direct(c)
 
-            if h == 0:
-                @pl.when(column == 0)
-                def _():
-                    for k in range(1, depth):
-                        table_to_row(lax.rem(d + k, depth)).start()
-                    for k in range(depth):
-                        table_to_mates(k).start()
+        @pl.when(late)
+        def _():
+            spread(0)
         return 0
 
     tiles_in.wait()
@@ -410,7 +429,7 @@
         arrived(held_s.at[pl.ds(0, depth - 1)], r_s.at[0])
         held = pltpu.make_async_copy(held_s.at[pl.ds(0, depth)], tables.at[0], s_l.at[0])
         held.start()
-        held.wait()
+        return held
 
     def total(c, slot, p):
         sf = got32[c, slot, p]
@@ -455,10 +474,12 @@
                     for q, value in enumerate(values):
                         out_ref[q // 2, q % 2, p, h * slab:(h + 1) * slab, lanes] = value
 
-    def other_tables():
+    def all_tables():
+        held = row_tables()
         arrived(held_s.at[pl.ds(0, depth)], r_s.at[1])
         more = pltpu.make_async_copy(held_s.at[pl.ds(depth, depth)], tables.at[1], s_l.at[1])
         more.start()
+        held.wait()
         more.wait()
 
     @pl.when(outer)
@@ -477,9 +498,9 @@
                 send_direct(chunk(i + 1))
             return 0
 
-        lax.fori_loop(0, chain, leaf, 0)
-        row_tables()
-        other_tables()
+        lax.fori_loop(1, chain, leaf, 0)
+        row_arrived(0)
+        all_tables()
 
         def own(i, _):
             c = chunk(i)
@@ -506,8 +527,7 @@
 
     @pl.when(inner)
     def _():
-        row_tables()
-        other_tables()
+        all_tables()
 
         def hub(i, _):
             c = chunk(i)

time: 37.1 us -> 37.1 us (level)
  no operation moved by 1% of the time
where the time goes in v5:
time: 37.1 us; the launch traced here: 37 us
  Pallas kernels  36.3 us (98%)
  between operations  0.64 us (2%)
    pallas_call x1, Pallas kernels, per_device(): pl.pallas_call(functools.partial(folded, depth), out_shape=jax.ShapeDtype...  35.5 us
    pallas_call x1, Pallas kernels, per_device(): pl.pallas_call(split, out_shape=(out, out), in_specs=[vmem], out_specs=(h...  0.79 us

profile of v5, /device:TPU:0, one launch (start us, length us, event | category | flops | bytes accessed | tf_op | source)
XLA Modules:
  0.0 37.0 jit_solution(5777027811897705117)
XLA Ops:
  0.6 35.5 %shard_map.68.both_ref = f32[2,2,4,16,512]{4,3,2,1,0:T(8,128)S(1)} custom-call(f32[4]{0:T(128)} %scale_hbm.1, s32[4,4]{1,0:T(4,128)} %lists_hbm.1, bf16[4,256,512]{2,1,0:T(8,128)(2,1)} %bitcast.2, bf16[4,512,512]{2,1,0:T(8,128)(2,1)} %matrix_hbm.1, s32[16,4,512]{2,1,0:T(4,128)} %bitcast.3), custom_call_target="tpu_custom_call" | custom-call | tf_op jit(solution)/shard_map/pallas_call | solution.py:626
  36.2 0.8 %shard_map.69 = (f32[2,4,16,512]{3,2,1,0:T(8,128)}, f32[2,4,16,512]{3,2,1,0:T(8,128)}) custom-call(f32[2,2,4,16,512]{4,3,2,1,0:T(8,128)S(1)} %shard_map.68.both_ref), custom_call_target="tpu_custom_call" | custom-call | tf_op jit(solution)/shard_map/pallas_call | solution.py:658

commit v6 on v5

--- a/solution.py
+++ b/solution.py
@@ -13,8 +13,8 @@
 MESH = pl.DeviceIdType.MESH
 STEP = 4
 LAG = 5
-LEAD = 5
-PRE = 5
+LEAD = 6
+PRE = 6
 SLAB = 4
 PIECES = 8
 SWAP = 3

time: 37.1 us -> 37.4 us (level)
  no operation moved by 1% of the time
where the time goes in v6:
time: 37.4 us; the launch traced here: 37.2 us
  Pallas kernels  36.6 us (98%)
  between operations  0.64 us (2%)
    pallas_call x1, Pallas kernels, per_device(): pl.pallas_call(functools.partial(folded, depth), out_shape=jax.ShapeDtype...  35.8 us
    pallas_call x1, Pallas kernels, per_device(): pl.pallas_call(split, out_shape=(out, out), in_specs=[vmem], out_specs=(h...  0.79 us

profile of v6, /device:TPU:0, one launch (start us, length us, event | category | flops | bytes accessed | tf_op | source)
XLA Modules:
  0.0 37.2 jit_solution(5836852606526489399)
XLA Ops:
  0.6 35.8 %shard_map.68.both_ref = f32[2,2,4,16,512]{4,3,2,1,0:T(8,128)S(1)} custom-call(f32[4]{0:T(128)} %scale_hbm.1, s32[4,4]{1,0:T(4,128)} %lists_hbm.1, bf16[4,256,512]{2,1,0:T(8,128)(2,1)} %bitcast.2, bf16[4,512,512]{2,1,0:T(8,128)(2,1)} %matrix_hbm.1, s32[16,4,512]{2,1,0:T(4,128)} %bitcast.3), custom_call_target="tpu_custom_call" | custom-call | tf_op jit(solution)/shard_map/pallas_call | solution.py:626
  36.4 0.8 %shard_map.69 = (f32[2,4,16,512]{3,2,1,0:T(8,128)}, f32[2,4,16,512]{3,2,1,0:T(8,128)}) custom-call(f32[2,2,4,16,512]{4,3,2,1,0:T(8,128)S(1)} %shard_map.68.both_ref), custom_call_target="tpu_custom_call" | custom-call | tf_op jit(solution)/shard_map/pallas_call | solution.py:658
